TPU v7x, 1024 devices: a whole 4x8x16 slice. The times are simulated.
1024 devices in a mesh: grp: 16 (over z), ep: 64 (over y, x, core).
Axes of the slice: x: 4, y: 8, z: 16, core: 2. Of those that a mesh axis runs over, the one named last changes fastest.
Arguments:
- hidden: bfloat16 [16, 64, 256, 1024], P('grp', 'ep'), may hold values from -6 to 6
- down_weight: bfloat16 [64, 1024, 4096], P('ep'), may hold values from -0.1875 to 0.1875
- slot_gate: float32 [16, 64, 256], P('grp', 'ep'), may hold values from 0.02 to 0.6
- slot_owner: int32 [16, 64, 256], P('grp', 'ep'), may hold values from 0 to 15
- slot_row: int32 [16, 64, 256], P('grp', 'ep'), may hold values from 0 to 31
- block_count: int32 [16, 64, 64], P('grp', 'ep'), may hold values from 0 to 4, as said below
Outputs:
- mixed: bfloat16 [32768, 4096], P(('grp', 'ep'))
Inputs may be any that keep to these rules, and one draw needn't show every extreme that they name: `block_count`: every device's expert has at least one block with all 4 slots live.
All inputs are finite; a program needn't handle non-finite values.
Results may differ from a plain program's by a relative error of at most 0.009.
Values may be sent and summed in bfloat16 or wider, within the bound.
No kernel may reach another device: no remote copies, remote signals or barrier semaphores. Data moves between devices by JAX's collectives and lax.ppermute only.
A program may use at most 64 MiB of HBM per device.

v0:
```python
import jax
import jax.numpy as jnp
from jax import lax
from jax.sharding import PartitionSpec as P

TOK_DEV = 32


def body(hidden, down_weight, slot_gate, slot_owner, slot_row, block_count):
    columns = lax.axis_size("ep")
    slot_total = hidden.shape[2]
    send = slot_total // columns
    product = jnp.dot(hidden[0, 0], down_weight[0], preferred_element_type=jnp.float32)
    within = jnp.arange(slot_total) % send
    limits = jnp.repeat(block_count[0, 0], send)
    live = (within < limits).astype(jnp.float32)
    scaled = (product * (slot_gate[0, 0] * live)[:, None]).astype(jnp.bfloat16)
    local_index = slot_owner[0, 0] * TOK_DEV + slot_row[0, 0]
    arrived, arrived_index = (
        lax.all_to_all(scaled, "ep", split_axis=0, concat_axis=0, tiled=True),
        lax.all_to_all(local_index, "ep", split_axis=0, concat_axis=0, tiled=True),
    )
    wanted = jnp.arange(lax.axis_size("grp") * TOK_DEV)
    table = (wanted[:, None] == arrived_index[None, :]).astype(jnp.bfloat16)
    return lax.psum_scatter(
        jnp.dot(table, arrived, preferred_element_type=jnp.float32).astype(jnp.bfloat16),
        "grp",
        scatter_dimension=0,
        tiled=True,
    )


def solution(mesh):
    in_specs = (
        P("grp", "ep", None, None),
        P("ep", None, None),
        P("grp", "ep", None),
        P("grp", "ep", None),
        P("grp", "ep", None),
        P("grp", "ep", None),
    )
    out_specs = P(("grp", "ep"), None)
    return jax.shard_map(body, mesh=mesh, in_specs=in_specs, out_specs=out_specs, check_vma=False)
```

profile of v0, /device:TPU:2, one launch (start us, length us, event | category | flops | bytes accessed | tf_op | source)
XLA Modules:
  0.0 191.0 jit_solution(2141292136162233446)
XLA Ops:
  6.5 0.0 copy-start
  6.5 0.8 add_reduce_fusion
  7.3 0.7 add.26
  8.0 17.2 %all-to-all-start = ((s32[64,4,1]{1,2,0:T(1,128)}), s32[64,4,1]{1,2,0:T(1,128)S(1)}, u32[]{:S(2)}, u32[]{:S(2)}) async-start(s32[64,4,1]{1,2,0:T(1,128)} %bitcast), calls=%async_computation | async-start | bytes 65536 | tf_op jit(solution)/shard_map/all_to_all | solution.py:21
  25.2 0.7 broadcast_in_dim.2
  26.0 0.1 reshape.51
  26.1 0.7 compare_select_fusion
  26.8 0.0 copy-done
  26.8 5.7 %fusion.5 = bf16[256,4096]{1,0:T(8,128)(2,1)S(1)} fusion(bf16[1,1024,4096]{2,1,0:T(8,128)(2,1)} %param.7, f32[256]{0:T(256)S(1)} %compare_select_fusion, bf16[1,1,256,1024]{3,2,1,0:T(8,128)(2,1)S(1)} %copy-done), kind=kOutput, calls=%fused_computation.4 | convolution fusion | flops 2149580800 | bytes 11011072 | tf_op jit(solution)/shard_map/dot_general | solution.py:13
  32.5 2.2 %all_to_all.13 = bf16[64,4,4096]{2,1,0:T(4,128)(2,1)} reshape(bf16[256,4096]{1,0:T(8,128)(2,1)S(1)} %fusion.5) | data formatting | bytes 4194304 | tf_op jit(solution)/shard_map/all_to_all | solution.py:20
  34.7 0.0 all-to-all-done
  34.7 10.4 %all-to-all-start.1 = ((bf16[64,4,4096]{2,1,0:T(4,128)(2,1)}), bf16[64,4,4096]{2,1,0:T(4,128)(2,1)S(1)}, u32[]{:S(2)}, u32[]{:S(2)}) async-start(bf16[64,4,4096]{2,1,0:T(4,128)(2,1)} %all_to_all.13), calls=%async_computation.1 | async-start | bytes 4194304 | tf_op jit(solution)/shard_map/all_to_all | solution.py:20
  45.1 0.0 reduce-scatter.2.cloned.1.call-start
  45.2 0.5 broadcast.45
  45.7 0.7 reduce.7
  46.4 0.1 eq.18
  46.5 49.8 %all-to-all-done.1 = bf16[64,4,4096]{2,1,0:T(4,128)(2,1)S(1)} async-done(((bf16[64,4,4096]{2,1,0:T(4,128)(2,1)}), bf16[64,4,4096]{2,1,0:T(4,128)(2,1)S(1)}, u32[]{:S(2)}, u32[]{:S(2)}) %all-to-all-start.1) | async-done | bytes 2097184 | tf_op jit(solution)/shard_map/all_to_all | solution.py:20
  96.4 2.1 %all_to_all.15 = bf16[256,4096]{1,0:T(8,128)(2,1)} reshape(bf16[64,4,4096]{2,1,0:T(4,128)(2,1)S(1)} %all-to-all-done.1) | data formatting | bytes 4194304 | tf_op jit(solution)/shard_map/all_to_all | solution.py:20
  98.4 4.8 %convolution_convert_fusion = bf16[512,4096]{1,0:T(8,128)(2,1)} fusion(bf16[256,4096]{1,0:T(8,128)(2,1)} %all_to_all.15, s32[256]{0:T(256)S(1)} %eq.18), kind=kOutput, calls=%fused_computation.2 | convolution fusion | flops 1075970048 | bytes 6292480 | tf_op jit(solution)/shard_map/dot_general | solution.py:26
  103.2 0.0 reduce-scatter.2.cloned.1.call-update
  103.2 81.0 %reduce-scatter.2.cloned.1.call-done = bf16[32,4096]{1,0:T(8,128)(2,1)} async-done(((bf16[512,4096]{1,0:T(8,128)(2,1)}), bf16[32,4096]{1,0:T(8,128)(2,1)}) %reduce-scatter.2.cloned.1.call-update) | async-done | bytes 262160 | tf_op jit(solution)/shard_map/reduce_scatter | solution.py:25
Async XLA Ops:
  6.5 20.2 %copy-start = (bf16[1,1,256,1024]{3,2,1,0:T(8,128)(2,1)S(1)}, bf16[1,1,256,1024]{3,2,1,0:T(8,128)(2,1)}, u32[]{:S(2)}) copy-start(bf16[1,1,256,1024]{3,2,1,0:T(8,128)(2,1)} %param.6) | copy-start | bytes 1572868
  8.0 26.7 %all-to-all-start = ((s32[64,4,1]{1,2,0:T(1,128)}), s32[64,4,1]{1,2,0:T(1,128)S(1)}, u32[]{:S(2)}, u32[]{:S(2)}) async-start(s32[64,4,1]{1,2,0:T(1,128)} %bitcast), calls=%async_computation | async-start | bytes 65536 | tf_op jit(solution)/shard_map/all_to_all | solution.py:21
  34.7 61.6 %all-to-all-start.1 = ((bf16[64,4,4096]{2,1,0:T(4,128)(2,1)}), bf16[64,4,4096]{2,1,0:T(4,128)(2,1)S(1)}, u32[]{:S(2)}, u32[]{:S(2)}) async-start(bf16[64,4,4096]{2,1,0:T(4,128)(2,1)} %all_to_all.13), calls=%async_computation.1 | async-start | bytes 4194304 | tf_op jit(solution)/shard_map/all_to_all | solution.py:20
  45.1 139.0 %reduce-scatter.2.cloned.1.call-start = ((), (), s32[]{:S(2)}) async-start(), calls=%async_computation.3 | async-start | bytes 4456448 | tf_op jit(solution)/shard_map/reduce_scatter | solution.py:25
Sparse Core Ops, SparseCore 0:
  103.3 80.7 reduce-scatter.1
where the time goes:
time: 191 us
  waiting for transfers between devices  131 us (69%)
  starting transfers between devices  27.6 us (14%)
  between operations  13.4 us (7%)
  matrix products  10.5 us (5%)
  local copies, waits for them, and re-layouts  6.46 us (3%)
  other arithmetic  2.18 us (1%)
    reduce_scatter x1, waiting for transfers between devices, body(): lax.psum_scatter(jnp.dot(table, arrived, preferred_element_type=jnp.float...  81 us
    all_to_all x1, waiting for transfers between devices, body(): lax.all_to_all(scaled, 'ep', split_axis=0, concat_axis=0, tiled=True)  49.8 us
    all_to_all x1, starting transfers between devices, body(): lax.all_to_all(local_index, 'ep', split_axis=0, concat_axis=0, tiled=True)  17.2 us
    all_to_all x1, starting transfers between devices, body(): lax.all_to_all(scaled, 'ep', split_axis=0, concat_axis=0, tiled=True)  10.4 us
    dot_general x1, matrix products, body(): jnp.dot(hidden[0, 0], down_weight[0], preferred_element_type=jnp.float32)  5.72 us
    dot_general x1, matrix products, body(): jnp.dot(table, arrived, preferred_element_type=jnp.float32)  4.77 us
    all_to_all x2, local copies, waits for them, and re-layouts, body(): lax.all_to_all(scaled, 'ep', split_axis=0, concat_axis=0, tiled=True)  4.28 us
  transfers between devices with their start and end apart: 3, of which 2 were waited for; matrix products, arithmetic and copies ran while one was open for 4% of the time, Pallas kernels for 0%

commit v1 on v0

v1 whole, which is shorter than its diff:
```python
import jax
import jax.numpy as jnp
from jax import lax
from jax.sharding import PartitionSpec as P

TOK_DEV = 32


def body(hidden, down_weight, slot_gate, slot_owner, slot_row, block_count):
    planes = lax.axis_size("grp")
    columns = lax.axis_size("ep")
    per_plane = columns // planes
    slot_total = hidden.shape[2]
    width = down_weight.shape[2]
    send = slot_total // columns
    bundle = slot_total // planes
    strip = width // planes
    tokens = planes * TOK_DEV

    within = jnp.arange(slot_total) % send
    limits = jnp.repeat(block_count[0, 0], send)
    live = (within < limits).astype(jnp.float32)
    scale = slot_gate[0, 0] * live
    index = slot_owner[0, 0] * TOK_DEV + slot_row[0, 0]

    rows = lax.all_to_all(hidden[0, 0], "grp", split_axis=0, concat_axis=0, tiled=True)
    notes = jnp.concatenate(
        [scale.reshape(planes, bundle), index.astype(jnp.float32).reshape(planes, bundle)], axis=1
    )
    notes = lax.all_to_all(notes, "grp", split_axis=0, concat_axis=0, tiled=True)

    def by_column(value):
        return value.reshape((planes, per_plane, send) + value.shape[2:]).swapaxes(0, 1)

    scale = by_column(notes[:, :bundle]).reshape(slot_total)
    index = by_column(notes[:, bundle:]).reshape(per_plane, planes * send)
    index = jnp.broadcast_to(index[None], (planes, per_plane, planes * send)).reshape(columns, planes * send)
    index = lax.all_to_all(index, "ep", split_axis=0, concat_axis=0, tiled=True).reshape(-1)

    rows = by_column(rows.reshape(planes, bundle, -1)).reshape(slot_total, -1)
    product = jnp.dot(rows, down_weight[0], preferred_element_type=jnp.float32)
    scaled = (product * scale[:, None]).astype(jnp.bfloat16)
    scaled = scaled.reshape(slot_total, planes, strip).swapaxes(0, 1).reshape(planes * slot_total, strip)
    arrived = lax.all_to_all(scaled, "ep", split_axis=0, concat_axis=0, tiled=True)

    wanted = jnp.arange(tokens).astype(jnp.float32)
    table = (wanted[:, None] == index[None, :]).astype(jnp.bfloat16)
    summed = jnp.dot(table, arrived, preferred_element_type=jnp.float32).astype(jnp.bfloat16)

    summed = lax.all_to_all(summed, "grp", split_axis=0, concat_axis=0, tiled=True)
    siblings = [[d * per_plane + k for d in range(planes)] for k in range(per_plane)]
    summed = lax.all_to_all(summed, "ep", split_axis=0, concat_axis=0, tiled=True, axis_index_groups=siblings)
    return summed.reshape(planes, TOK_DEV, strip).swapaxes(0, 1).reshape(TOK_DEV, width)


def solution(mesh):
    in_specs = (
        P("grp", "ep", None, None),
        P("ep", None, None),
        P("grp", "ep", None),
        P("grp", "ep", None),
        P("grp", "ep", None),
        P("grp", "ep", None),
    )
    out_specs = P(("grp", "ep"), None)
    return jax.shard_map(body, mesh=mesh, in_specs=in_specs, out_specs=out_specs, check_vma=False)
```

time: 191 us -> 192 us (level)
  the two profiles are of different devices: /device:TPU:2 before, /device:TPU:64 now
where the time goes in v1:
time: 192 us; the launch traced here: 191 us
  waiting for transfers between devices  79.1 us (41%)
  blocking collectives  71.1 us (37%)
  starting transfers between devices  24.2 us (13%)
  matrix products  7.03 us (4%)
  local copies, waits for them, and re-layouts  5.87 us (3%)
  other arithmetic  4.07 us (2%)
    all_to_all x1, waiting for transfers between devices, body(): lax.all_to_all(scaled, 'ep', split_axis=0, concat_axis=0, tiled=True)  50.5 us
    all_to_all x1, blocking collectives, body(): lax.all_to_all(notes, 'grp', split_axis=0, concat_axis=0, tiled=True)  29.4 us
    all_to_all x1, waiting for transfers between devices, body(): lax.all_to_all(hidden[0, 0], 'grp', split_axis=0, concat_axis=0, tiled=True)  27.2 us
    all_to_all x1, blocking collectives, body(): lax.all_to_all(summed, 'grp', split_axis=0, concat_axis=0, tiled=True)  24.1 us
    all_to_all x1, blocking collectives, body(): lax.all_to_all(summed, 'ep', split_axis=0, concat_axis=0, tiled=True, axi...  17.6 us
    all_to_all x1, starting transfers between devices, body(): lax.all_to_all(index, 'ep', split_axis=0, concat_axis=0, tiled=True)  10.6 us
    all_to_all x1, starting transfers between devices, body(): lax.all_to_all(scaled, 'ep', split_axis=0, concat_axis=0, tiled=True)  8.89 us
    dot_general x1, matrix products, body(): product = jnp.dot(rows, down_weight[0], preferred_element_type=jnp.float32)  5.73 us
  transfers between devices with their start and end apart: 3, of which 3 were waited for; matrix products, arithmetic and copies ran while one was open for 5% of the time, Pallas kernels for 0%

profile of v1, /device:TPU:64, one launch (start us, length us, event | category | flops | bytes accessed | tf_op | source)
XLA Modules:
  0.0 191.5 jit_solution(8892571399591196735)
XLA Ops:
  0.0 0.7 convert_reduce_fusion
  0.9 0.5 broadcast.36
  1.4 1.3 reduce.13
  2.9 0.5 broadcast.37
  3.4 1.3 reduce.14
  5.0 29.4 %all_to_all.57 = f32[16,1,32]{2,1,0:T(1,128)S(1)} all-to-all(f32[16,1,32]{2,1,0:T(1,128)S(1)} %copy.33), channel_id=1, replica_groups=mesh['grp'=16,'ep'=64] {'grp'}, dimensions={0} | all-to-all | bytes 4096 | tf_op jit(solution)/shard_map/all_to_all | solution.py:30
  34.3 4.8 %all-to-all-start.2 = ((bf16[16,16,1024]{2,1,0:T(8,128)(2,1)}), bf16[16,16,1024]{2,1,0:T(8,128)(2,1)S(1)}, u32[]{:S(2)}, u32[]{:S(2)}) async-start(bf16[16,16,1024]{2,1,0:T(8,128)(2,1)} %bitcast.40), calls=%async_computation.2 | async-start | bytes 1048576 | tf_op jit(solution)/shard_map/all_to_all | solution.py:26
  39.3 0.1 mul.24
  39.6 27.2 %all-to-all-done.2 = bf16[16,16,1024]{2,1,0:T(8,128)(2,1)S(1)} async-done(((bf16[16,16,1024]{2,1,0:T(8,128)(2,1)}), bf16[16,16,1024]{2,1,0:T(8,128)(2,1)S(1)}, u32[]{:S(2)}, u32[]{:S(2)}) %all-to-all-start.2) | async-done | bytes 524320 | tf_op jit(solution)/shard_map/all_to_all | solution.py:26
  66.8 0.6 broadcast_in_dim.19
  67.4 10.6 %all-to-all-start.1 = ((f32[64,1,64]{2,1,0:T(1,128)}), f32[64,1,64]{2,1,0:T(1,128)S(1)}, u32[]{:S(2)}, u32[]{:S(2)}) async-start(f32[64,1,64]{2,1,0:T(1,128)} %bitcast.5), calls=%async_computation.1 | async-start | bytes 65536 | tf_op jit(solution)/shard_map/all_to_all | solution.py:38
  78.0 0.3 copy.36
  78.3 0.4 copy.37
  78.7 0.1 reshape.60
  78.8 5.7 %fusion.7 = bf16[256,4096]{1,0:T(8,128)(2,1)S(1)} fusion(bf16[256,1024]{1,0:T(8,128)(2,1)S(1)} %reshape.60, bf16[1,1024,4096]{2,1,0:T(8,128)(2,1)} %param.7, f32[256]{0:T(256)S(1)} %mul.24), kind=kOutput, calls=%fused_computation.5 | convolution fusion | flops 2149580800 | bytes 11011072 | tf_op jit(solution)/shard_map/dot_general | solution.py:41
  84.5 1.6 copy.44
  86.1 1.4 all-to-all-done.1
  87.5 8.9 %all-to-all-start.3 = ((bf16[64,64,256]{2,1,0:T(8,128)(2,1)}), bf16[64,64,256]{2,1,0:T(8,128)(2,1)S(1)}, u32[]{:S(2)}, u32[]{:S(2)}) async-start(bf16[64,64,256]{2,1,0:T(8,128)(2,1)} %bitcast.13), calls=%async_computation.3 | async-start | bytes 4194304 | tf_op jit(solution)/shard_map/all_to_all | solution.py:44
  96.4 0.7 reduce.15
  97.2 50.5 %all-to-all-done.3 = bf16[64,64,256]{2,1,0:T(8,128)(2,1)S(1)} async-done(((bf16[64,64,256]{2,1,0:T(8,128)(2,1)}), bf16[64,64,256]{2,1,0:T(8,128)(2,1)S(1)}, u32[]{:S(2)}, u32[]{:S(2)}) %all-to-all-start.3) | async-done | bytes 2097184 | tf_op jit(solution)/shard_map/all_to_all | solution.py:44
  147.7 1.3 fusion.12
  149.1 24.1 %all_to_all.58 = bf16[16,32,256]{2,1,0:T(8,128)(2,1)S(1)} all-to-all(bf16[16,32,256]{2,1,0:T(8,128)(2,1)S(1)} %bitcast.41), channel_id=1, replica_groups=mesh['grp'=16,'ep'=64] {'grp'}, dimensions={0} | all-to-all | bytes 524288 | tf_op jit(solution)/shard_map/all_to_all | solution.py:50
  173.2 17.6 %all_to_all.59 = bf16[16,32,256]{2,1,0:T(8,128)(2,1)S(1)} all-to-all(bf16[16,32,256]{2,1,0:T(8,128)(2,1)S(1)} %all_to_all.58), channel_id=1, replica_groups={{0,4,8,12,16,20,24,28,32,36,40,44,48,52,56,60},{1,5,9,13,17,21,25,29,33..., dimensions={0} | all-to-all | bytes 524288 | tf_op jit(solution)/shard_map/all_to_all | solution.py:52
  190.8 0.7 copy.42
  (17 shorter events, 1.0 us)
Async XLA Ops:
  34.3 32.4 %all-to-all-start.2 = ((bf16[16,16,1024]{2,1,0:T(8,128)(2,1)}), bf16[16,16,1024]{2,1,0:T(8,128)(2,1)S(1)}, u32[]{:S(2)}, u32[]{:S(2)}) async-start(bf16[16,16,1024]{2,1,0:T(8,128)(2,1)} %bitcast.40), calls=%async_computation.2 | async-start | bytes 1048576 | tf_op jit(solution)/shard_map/all_to_all | solution.py:26
  67.4 20.1 %all-to-all-start.1 = ((f32[64,1,64]{2,1,0:T(1,128)}), f32[64,1,64]{2,1,0:T(1,128)S(1)}, u32[]{:S(2)}, u32[]{:S(2)}) async-start(f32[64,1,64]{2,1,0:T(1,128)} %bitcast.5), calls=%async_computation.1 | async-start | bytes 65536 | tf_op jit(solution)/shard_map/all_to_all | solution.py:38
  87.5 60.2 %all-to-all-start.3 = ((bf16[64,64,256]{2,1,0:T(8,128)(2,1)}), bf16[64,64,256]{2,1,0:T(8,128)(2,1)S(1)}, u32[]{:S(2)}, u32[]{:S(2)}) async-start(bf16[64,64,256]{2,1,0:T(8,128)(2,1)} %bitcast.13), calls=%async_computation.3 | async-start | bytes 4194304 | tf_op jit(solution)/shard_map/all_to_all | solution.py:44

commit v2 on v1

v2 whole, which is shorter than its diff:
```python
import jax
import jax.numpy as jnp
from jax import lax
from jax.experimental import pallas as pl
from jax.experimental.pallas import tpu as pltpu
from jax.sharding import PartitionSpec as P

TOK_DEV = 32


def exchange(value, axis, groups=None):
    return lax.all_to_all(value, axis, split_axis=0, concat_axis=0, tiled=True, axis_index_groups=groups)


def scale_kernel(send, gate_ref, count_ref, hidden_ref, out_ref):
    slots, columns = hidden_ref.shape[0], count_ref.shape[1]
    slot = lax.broadcasted_iota(jnp.int32, (slots, 1), 0)
    own = slot == lax.broadcasted_iota(jnp.int32, (slots, slots), 1)
    gate = jnp.sum(jnp.where(own, gate_ref[...], 0.0), axis=1, keepdims=True)
    block = slot // send == lax.broadcasted_iota(jnp.int32, (slots, columns), 1)
    limit = jnp.sum(jnp.where(block, count_ref[...], 0).astype(jnp.float32), axis=1, keepdims=True)
    scale = jnp.where((slot % send).astype(jnp.float32) < limit, gate, 0.0)
    out_ref[...] = (hidden_ref[...].astype(jnp.float32) * scale).astype(jnp.bfloat16)


def scaled_rows(hidden, gate, count, send):
    return pl.pallas_call(
        lambda *refs: scale_kernel(send, *refs),
        out_shape=jax.ShapeDtypeStruct(hidden.shape, jnp.bfloat16),
        cost_estimate=pl.CostEstimate(flops=2 * hidden.size, bytes_accessed=4 * hidden.size, transcendentals=0),
        name="scaled_rows",
    )(gate, count, hidden)


def product_kernel(strip, mates, send, rows_ref, weight_ref, out_ref, sorted_ref):
    count = rows_ref.shape[0]
    block = out_ref.shape[0] // count * strip

    @pl.when(pl.program_id(0) == 0)
    def _():
        place = lax.broadcasted_iota(jnp.int32, (count, count), 0)
        source = lax.broadcasted_iota(jnp.int32, (count, count), 1)
        groups = count // (mates * send)
        mate, group, slot = place // (groups * send), (place // send) % groups, place % send
        move = (source == (group * mates + mate) * send + slot).astype(jnp.float32).astype(jnp.bfloat16)
        sorted_ref[...] = jnp.dot(move, rows_ref[...], preferred_element_type=jnp.float32).astype(jnp.bfloat16)

    product = jnp.dot(sorted_ref[...], weight_ref[...], preferred_element_type=jnp.float32).astype(jnp.bfloat16)
    for i in range(block // strip):
        out_ref[i * count : (i + 1) * count, :] = product[:, i * strip : (i + 1) * strip]


def strip_product(rows, weight, strip, mates, send):
    count, depth = rows.shape
    width = weight.shape[1]
    block = 2 * strip
    return pl.pallas_call(
        lambda *refs: product_kernel(strip, mates, send, *refs),
        grid=(width // block,),
        out_shape=jax.ShapeDtypeStruct((width // strip * count, strip), jnp.bfloat16),
        in_specs=[pl.BlockSpec(memory_space=pltpu.VMEM), pl.BlockSpec((depth, block), lambda i: (0, i))],
        out_specs=pl.BlockSpec((block // strip * count, strip), lambda i: (i, 0)),
        scratch_shapes=[pltpu.VMEM((count, depth), jnp.bfloat16)],
        cost_estimate=pl.CostEstimate(
            flops=2 * count * depth * width, bytes_accessed=2 * (depth + count) * width, transcendentals=0
        ),
        name="strip_product",
    )(rows, weight)


def body(hidden, down_weight, slot_gate, slot_owner, slot_row, block_count):
    planes = lax.axis_size("grp")
    columns = lax.axis_size("ep")
    slot_total, _ = hidden.shape[2:]
    width = down_weight.shape[2]
    mates = columns // planes
    send = slot_total // columns
    strip = width // planes
    tokens = planes * TOK_DEV

    rows = scaled_rows(hidden[0, 0], slot_gate[0], block_count[0], send)
    rows = exchange(rows, "grp")

    mate = lax.axis_index("ep") % mates
    index = slot_owner[0, 0] * TOK_DEV + slot_row[0, 0]
    index = lax.all_gather(index, "ep", axis=0)
    index = index.reshape(columns, planes, mates, send)
    index = lax.dynamic_index_in_dim(index, mate, axis=2, keepdims=False).swapaxes(0, 1)
    index = index.reshape(planes, columns * send)

    product = strip_product(rows, down_weight[0], strip, mates, send)
    arrived = exchange(product, "ep")

    index = lax.all_gather(index, "grp", axis=0)
    index = lax.dynamic_index_in_dim(index, lax.axis_index("grp"), axis=1, keepdims=False)
    index = index.reshape(planes, columns, send).swapaxes(0, 1).reshape(-1)

    wanted = jnp.arange(tokens)
    table = (wanted[:, None] == index[None, :]).astype(jnp.bfloat16)
    summed = jnp.dot(table, arrived, preferred_element_type=jnp.float32).astype(jnp.bfloat16)

    summed = exchange(summed, "grp")
    siblings = [[d * mates + k for d in range(planes)] for k in range(mates)]
    summed = exchange(summed, "ep", siblings)
    return summed.reshape(planes, TOK_DEV, strip).swapaxes(0, 1).reshape(TOK_DEV, width)


def solution(mesh):
    in_specs = (
        P("grp", "ep", None, None),
        P("ep", None, None),
        P("grp", "ep", None),
        P("grp", "ep", None),
        P("grp", "ep", None),
        P("grp", "ep", None),
    )
    out_specs = P(("grp", "ep"), None)
    return jax.shard_map(body, mesh=mesh, in_specs=in_specs, out_specs=out_specs, check_vma=False)
```

time: 192 us -> 223 us (1.16)
  blocking collectives: 71.1 us -> 198 us
  waiting for transfers between devices: 79.1 us -> 0.01 us
  starting transfers between devices: 24.2 us -> 10.7 us
  Pallas kernels: 0 us -> 11 us
  matrix products: 7.03 us -> 1.36 us
  other arithmetic: 4.07 us -> 0.01 us
  local copies, waits for them, and re-layouts: 5.87 us -> 1.85 us
    all_gather x0 -> x2, blocking collectives: none -> 109 us  [the longest x1 79.8 us: body(): index = lax.all_gather(index, 'ep', axis=0)]
    all_to_all x3 -> x1, waiting for transfers between devices: 79.1 us -> 0.01 us  [exchange(): lax.all_to_all(value, axis, split_axis=0, concat_axis=0, tiled=True, axis...]
    all_to_all x3, blocking collectives: 71.1 us -> 88.6 us  [exchange(): lax.all_to_all(value, axis, split_axis=0, concat_axis=0, tiled=True, axis...]
    all_to_all x3 -> x1, starting transfers between devices: 24.2 us -> 10.7 us  [exchange(): lax.all_to_all(value, axis, split_axis=0, concat_axis=0, tiled=True, axis...]
    pallas_call x0 -> x2, Pallas kernels: none -> 11 us  [the longest x1 8.94 us: strip_product(): pl.pallas_call(lambda *refs: product_kernel(strip, mates, send, *refs), g...]
    dot_general x1 -> x0, matrix products: 5.73 us -> none  [body(): product = jnp.dot(rows, down_weight[0], preferred_element_type=jnp.float32)]
    unnamed x2 -> x0, other arithmetic: 2.63 us -> none
  transfers between devices with their start and end apart: 3 -> 1, of which waited for: 3 -> 0; matrix products, arithmetic and copies ran while one was open for 5% -> 1% of each run, Pallas kernels for 0% -> 0%
where the time goes in v2:
time: 223 us
  blocking collectives  198 us (89%)
  Pallas kernels  11 us (5%)
  starting transfers between devices  10.7 us (5%)
    all_to_all x3, blocking collectives, exchange(): lax.all_to_all(value, axis, split_axis=0, concat_axis=0, tiled=True, axis...  88.6 us
    all_gather x1, blocking collectives, body(): index = lax.all_gather(index, 'ep', axis=0)  79.8 us
    all_gather x1, blocking collectives, body(): index = lax.all_gather(index, 'grp', axis=0)  29.3 us
    all_to_all x1, starting transfers between devices, exchange(): lax.all_to_all(value, axis, split_axis=0, concat_axis=0, tiled=True, axis...  10.7 us
    pallas_call x1, Pallas kernels, strip_product(): pl.pallas_call(lambda *refs: product_kernel(strip, mates, send, *refs), g...  8.94 us
  transfers between devices with their start and end apart: 1, of which 0 were waited for; matrix products, arithmetic and copies ran while one was open for 1% of the time, Pallas kernels for 0%

profile of v2, /device:TPU:64, one launch (start us, length us, event | category | flops | bytes accessed | tf_op | source)
XLA Modules:
  0.0 222.7 jit_solution(722869414168109466)
XLA Ops:
  0.0 2.1 scaled_rows.1
  2.1 47.0 %all_to_all.38 = bf16[16,16,1024]{2,1,0:T(8,128)(2,1)} all-to-all(bf16[16,16,1024]{2,1,0:T(8,128)(2,1)} %bitcast.26), channel_id=1, replica_groups=mesh['grp'=16,'ep'=64] {'grp'}, dimensions={0} | all-to-all | bytes 1048576 | tf_op jit(solution)/shard_map/all_to_all | solution.py:12
  49.1 8.9 %strip_product.1 = bf16[4096,256]{1,0:T(8,128)(2,1)} custom-call(bf16[256,1024]{1,0:T(8,128)(2,1)} %bitcast.27, bf16[1024,4096]{1,0:T(8,128)(2,1)} %bitcast.23), custom_call_target="tpu_custom_call" | custom-call | flops 2147483648 | bytes 10485760 | tf_op jit(solution)/shard_map/strip_product/pallas_call | solution.py:57
  58.0 0.0 copy-start
  58.0 0.0 copy-start.1
  58.0 10.7 %all-to-all-start.1 = ((bf16[64,64,256]{2,1,0:T(8,128)(2,1)}), bf16[64,64,256]{2,1,0:T(8,128)(2,1)S(1)}, u32[]{:S(2)}, u32[]{:S(2)}) async-start(bf16[64,64,256]{2,1,0:T(8,128)(2,1)} %bitcast.24), calls=%async_computation.1 | async-start | bytes 4194304 | tf_op jit(solution)/shard_map/all_to_all | solution.py:12
  68.8 0.0 copy-done
  68.8 0.0 copy-done.1
  68.8 79.8 %all-gather = s32[64,1,256]{2,1,0:T(1,128)S(1)} all-gather(s32[1,1,256]{2,1,0:T(1,128)S(1)} %multiply_add_fusion), channel_id=2, replica_groups=mesh['grp'=16,'ep'=64] {'ep'}, dimensions={0}, use_global_device_ids=true | all-gather | bytes 66560 | tf_op jit(solution)/shard_map/all_gather | solution.py:86
  148.6 0.1 copy.22
  148.7 0.1 copy.24
  148.8 0.1 copy.25
  148.9 29.3 %all_gather.8 = s32[16,16,256]{2,1,0:T(8,128)S(1)} all-gather(s32[1,16,256]{2,1,0:T(8,128)S(1)} %copy.25), channel_id=1, replica_groups=mesh['grp'=16,'ep'=64] {'grp'}, dimensions={0}, use_global_device_ids=true | all-gather | bytes 278528 | tf_op jit(solution)/shard_map/all_gather | solution.py:94
  178.2 0.1 copy.26
  178.3 0.4 copy.27
  178.7 0.3 eq.18
  179.0 0.0 all-to-all-done.1
  179.0 1.4 fusion.2
  180.4 22.3 %all_to_all.39 = bf16[16,32,256]{2,1,0:T(8,128)(2,1)S(1)} all-to-all(bf16[16,32,256]{2,1,0:T(8,128)(2,1)S(1)} %bitcast.32), channel_id=1, replica_groups=mesh['grp'=16,'ep'=64] {'grp'}, dimensions={0} | all-to-all | bytes 524288 | tf_op jit(solution)/shard_map/all_to_all | solution.py:12
  202.7 19.3 %all_to_all.40 = bf16[16,32,256]{2,1,0:T(8,128)(2,1)S(1)} all-to-all(bf16[16,32,256]{2,1,0:T(8,128)(2,1)S(1)} %all_to_all.39), channel_id=1, replica_groups={{0,4,8,12,16,20,24,28,32,36,40,44,48,52,56,60},{1,5,9,13,17,21,25,29,33..., dimensions={0} | all-to-all | bytes 524288 | tf_op jit(solution)/shard_map/all_to_all | solution.py:12
  222.0 0.7 copy.29
  (4 shorter events, 0.0 us)
Async XLA Ops:
  58.0 10.7 %copy-start = (s32[1,1,256]{2,1,0:T(1,128)S(1)}, s32[1,1,256]{2,1,0:T(1,128)}, u32[]{:S(2)}) copy-start(s32[1,1,256]{2,1,0:T(1,128)} %param.10) | copy-start | bytes 3076
  58.0 10.7 %copy-start.1 = (s32[1,1,256]{2,1,0:T(1,128)S(1)}, s32[1,1,256]{2,1,0:T(1,128)}, u32[]{:S(2)}) copy-start(s32[1,1,256]{2,1,0:T(1,128)} %param.9) | copy-start | bytes 3076
  58.0 121.0 %all-to-all-start.1 = ((bf16[64,64,256]{2,1,0:T(8,128)(2,1)}), bf16[64,64,256]{2,1,0:T(8,128)(2,1)S(1)}, u32[]{:S(2)}, u32[]{:S(2)}) async-start(bf16[64,64,256]{2,1,0:T(8,128)(2,1)} %bitcast.24), calls=%async_computation.1 | async-start | bytes 4194304 | tf_op jit(solution)/shard_map/all_to_all | solution.py:12

commit v3 on v2

v3 whole, which is shorter than its diff:
```python
import jax
import jax.numpy as jnp
from jax import lax
from jax.experimental import pallas as pl
from jax.experimental.pallas import tpu as pltpu
from jax.sharding import PartitionSpec as P

TOK_DEV = 32


def exchange(value, axis, groups=None):
    return lax.all_to_all(value, axis, split_axis=0, concat_axis=0, tiled=True, axis_index_groups=groups)


def moved(rows, source):
    pick = source == lax.broadcasted_iota(jnp.int32, source.shape, 1)
    pick = pick.astype(jnp.float32).astype(jnp.bfloat16)
    return jnp.dot(pick, rows, preferred_element_type=jnp.float32).astype(jnp.bfloat16)


def scale_kernel(planes, mates, send, gate_ref, count_ref, hidden_ref, out_ref):
    slots, columns = hidden_ref.shape[0], count_ref.shape[1]
    slot = lax.broadcasted_iota(jnp.int32, (slots, 1), 0)
    own = slot == lax.broadcasted_iota(jnp.int32, (slots, slots), 1)
    gate = jnp.sum(jnp.where(own, gate_ref[...], 0.0), axis=1, keepdims=True)
    block = slot // send == lax.broadcasted_iota(jnp.int32, (slots, columns), 1)
    limit = jnp.sum(jnp.where(block, count_ref[...], 0).astype(jnp.float32), axis=1, keepdims=True)
    scale = jnp.where((slot % send).astype(jnp.float32) < limit, gate, 0.0)
    scaled = (hidden_ref[...].astype(jnp.float32) * scale).astype(jnp.bfloat16)
    place = lax.broadcasted_iota(jnp.int32, (slots, slots), 0)
    plane, mate, slot = place // (mates * send), (place // send) % mates, place % send
    out_ref[...] = moved(scaled, (mate * planes + plane) * send + slot)


def scaled_rows(hidden, gate, count, planes, mates, send):
    return pl.pallas_call(
        lambda *refs: scale_kernel(planes, mates, send, *refs),
        out_shape=jax.ShapeDtypeStruct(hidden.shape, jnp.bfloat16),
        cost_estimate=pl.CostEstimate(flops=2 * hidden.size, bytes_accessed=4 * hidden.size, transcendentals=0),
        name="scaled_rows",
    )(gate, count, hidden)


def product_kernel(planes, mates, send, rows_ref, weight_ref, out_ref, weights, outs, in_sems, out_sems):
    count = rows_ref.shape[0]
    pieces, _, block = weights.shape
    strip = out_ref.shape[3]
    per = block // strip
    loads = [
        pltpu.make_async_copy(weight_ref.at[:, i * block : (i + 1) * block], weights.at[i], in_sems.at[i])
        for i in range(pieces)
    ]
    stores = [
        pltpu.make_async_copy(outs.at[:, i * per : (i + 1) * per], out_ref.at[:, i * per : (i + 1) * per], out_sems.at[i])
        for i in range(pieces)
    ]
    for load in loads:
        load.start()
    place = lax.broadcasted_iota(jnp.int32, (count, count), 0)
    mate, group, slot = place // (planes * send), (place // send) % planes, place % send
    rows = moved(rows_ref[...], (group * mates + mate) * send + slot)
    bundle = planes * send
    for i in range(pieces):
        loads[i].wait()
        product = jnp.dot(rows, weights[i], preferred_element_type=jnp.float32).astype(jnp.bfloat16)
        for j in range(per):
            for k in range(mates):
                outs[k, i * per + j] = product[k * bundle : (k + 1) * bundle, j * strip : (j + 1) * strip]
        if i:
            stores[i - 1].start()
    stores[-1].start()
    for store in stores:
        store.wait()


def strip_product(rows, weight, planes, mates, send):
    count, depth = rows.shape
    width = weight.shape[1]
    strip = width // planes
    block = 2 * strip
    pieces = width // block
    shape = (mates, planes, planes * send, strip)
    return pl.pallas_call(
        lambda *refs: product_kernel(planes, mates, send, *refs),
        out_shape=jax.ShapeDtypeStruct(shape, jnp.bfloat16),
        in_specs=[pl.BlockSpec(memory_space=pltpu.VMEM), pl.BlockSpec(memory_space=pltpu.HBM)],
        out_specs=pl.BlockSpec(memory_space=pltpu.HBM),
        scratch_shapes=[
            pltpu.VMEM((pieces, depth, block), jnp.bfloat16),
            pltpu.VMEM(shape, jnp.bfloat16),
            pltpu.SemaphoreType.DMA((pieces,)),
            pltpu.SemaphoreType.DMA((pieces,)),
        ],
        cost_estimate=pl.CostEstimate(
            flops=2 * count * depth * width, bytes_accessed=2 * (depth + count) * width, transcendentals=0
        ),
        compiler_params=pltpu.CompilerParams(vmem_limit_bytes=50 * 1024 * 1024),
        name="strip_product",
    )(rows, weight)


def gathered(index):
    columns = lax.axis_size("ep")
    near = min(8, columns // 2)
    groups = [[i * near + j for j in range(near)] for i in range(columns // near)]
    index = lax.all_gather(index, "ep", axis=0, axis_index_groups=groups)
    step = near
    while step < columns:
        upper = (lax.axis_index("ep") // step) % 2 == 1
        other = lax.ppermute(index, "ep", [(i, i ^ step) for i in range(columns)])
        low, high = jnp.where(upper, other, index), jnp.where(upper, index, other)
        index = jnp.concatenate([low, high], axis=0)
        step *= 2
    return index


def body(hidden, down_weight, slot_gate, slot_owner, slot_row, block_count):
    planes = lax.axis_size("grp")
    columns = lax.axis_size("ep")
    slot_total = hidden.shape[2]
    width = down_weight.shape[2]
    mates = columns // planes
    send = slot_total // columns
    strip = width // planes
    tokens = planes * TOK_DEV

    rows = scaled_rows(hidden[0, 0], slot_gate[0], block_count[0], planes, mates, send)
    rows = exchange(rows, "grp")

    index = slot_owner[0, 0] * TOK_DEV + slot_row[0, 0]
    index = gathered(index).reshape(columns, mates, planes, send)
    index = lax.dynamic_index_in_dim(index, lax.axis_index("ep") // planes, axis=1, keepdims=False)
    index = index.swapaxes(0, 1).reshape(planes, columns * send)

    product = strip_product(rows, down_weight[0], planes, mates, send)
    arrived = exchange(product.reshape(columns * planes * send, strip), "ep")

    index = lax.all_gather(index, "grp", axis=0)
    index = lax.dynamic_index_in_dim(index, lax.axis_index("grp"), axis=1, keepdims=False)
    index = index.reshape(planes, columns, send).swapaxes(0, 1).reshape(-1)

    wanted = jnp.arange(tokens)
    table = (wanted[:, None] == index[None, :]).astype(jnp.bfloat16)
    summed = jnp.dot(table, arrived, preferred_element_type=jnp.float32).astype(jnp.bfloat16)

    summed = exchange(summed, "grp")
    siblings = [[mate * planes + d for d in range(planes)] for mate in range(mates)]
    summed = exchange(summed, "ep", siblings)
    return summed.reshape(planes, TOK_DEV, strip).swapaxes(0, 1).reshape(TOK_DEV, width)


def solution(mesh):
    in_specs = (
        P("grp", "ep", None, None),
        P("ep", None, None),
        P("grp", "ep", None),
        P("grp", "ep", None),
        P("grp", "ep", None),
        P("grp", "ep", None),
    )
    out_specs = P(("grp", "ep"), None)
    return jax.shard_map(body, mesh=mesh, in_specs=in_specs, out_specs=out_specs, check_vma=False)
```

time: 223 us -> 200 us (0.90)
  the two profiles are of different devices: /device:TPU:64 before, /device:TPU:1 now
where the time goes in v3:
time: 200 us
  blocking collectives  120 us (60%)
  waiting for transfers between devices  38.9 us (19%)
  starting transfers between devices  29 us (14%)
  Pallas kernels  8.07 us (4%)
    all_to_all x3, blocking collectives, exchange(): lax.all_to_all(value, axis, split_axis=0, concat_axis=0, tiled=True, axis...  84.5 us
    ppermute x3, waiting for transfers between devices, gathered(): other = lax.ppermute(index, 'ep', [(i, i ^ step) for i in range(columns)])  38.9 us
    all_gather x1, blocking collectives, body(): index = lax.all_gather(index, 'grp', axis=0)  24.7 us
    all_to_all x1, starting transfers between devices, exchange(): lax.all_to_all(value, axis, split_axis=0, concat_axis=0, tiled=True, axis...  17.1 us
    ppermute x3, starting transfers between devices, gathered(): other = lax.ppermute(index, 'ep', [(i, i ^ step) for i in range(columns)])  11.9 us
    all_gather x1, blocking collectives, gathered(): index = lax.all_gather(index, 'ep', axis=0, axis_index_groups=groups)  10.9 us
    pallas_call x1, Pallas kernels, strip_product(): pl.pallas_call(lambda *refs: product_kernel(planes, mates, send, *refs),...  5.74 us
  transfers between devices with their start and end apart: 4, of which 3 were waited for; matrix products, arithmetic and copies ran while one was open for 1% of the time, Pallas kernels for 0%

profile of v3, /device:TPU:1, one launch (start us, length us, event | category | flops | bytes accessed | tf_op | source)
XLA Modules:
  0.0 199.8 jit_solution(16438105706156145223)
XLA Ops:
  0.0 2.3 %scaled_rows.1 = bf16[256,1024]{1,0:T(8,128)(2,1)} custom-call(f32[1,256]{1,0:T(1,128)} %bitcast.42, s32[1,64]{1,0:T(1,128)} %bitcast.43, bf16[256,1024]{1,0:T(8,128)(2,1)} %bitcast.37), custom_call_target="tpu_custom_call" | custom-call | flops 524288 | bytes 1048576 | tf_op jit(solution)/shard_map/scaled_rows/pallas_call | solution.py:36
  2.3 42.4 %all_to_all.38 = bf16[16,16,1024]{2,1,0:T(8,128)(2,1)S(1)} all-to-all(bf16[16,16,1024]{2,1,0:T(8,128)(2,1)} %bitcast.33), channel_id=1, replica_groups=mesh['grp'=16,'ep'=64] {'grp'}, dimensions={0} | all-to-all | bytes 1048576 | tf_op jit(solution)/shard_map/all_to_all | solution.py:12
  44.7 5.7 %strip_product.1 = bf16[4,16,64,256]{3,2,1,0:T(8,128)(2,1)} custom-call(bf16[256,1024]{1,0:T(8,128)(2,1)S(1)} %bitcast.30, bf16[1024,4096]{1,0:T(8,128)(2,1)} %bitcast.31), custom_call_target="tpu_custom_call" | custom-call | flops 2147483648 | bytes 10485760 | tf_op jit(solution)/shard_map/strip_product/pallas_call | solution.py:83
  50.5 0.0 copy-start
  50.5 17.1 %all-to-all-start.1 = ((bf16[64,64,256]{2,1,0:T(8,128)(2,1)}), bf16[64,64,256]{2,1,0:T(8,128)(2,1)S(1)}, u32[]{:S(2)}, u32[]{:S(2)}) async-start(bf16[64,64,256]{2,1,0:T(8,128)(2,1)} %bitcast.12), calls=%async_computation.1 | async-start | bytes 4194304 | tf_op jit(solution)/shard_map/all_to_all | solution.py:12
  67.7 10.9 %all-gather = s32[8,1,256]{2,1,0:T(1,128)S(1)} all-gather(s32[1,1,256]{2,1,0:T(1,128)S(1)} %multiply_add_fusion), channel_id=2, replica_groups={{0,1,2,3,4,5,6,7},{8,9,10,11,12,13,14,15},{16,17,18,19,20,21,22,23},{24..., dimensions={0}, use_global_device_ids=true | all-gather | bytes 9216 | tf_op jit(solution)/shard_map/all_gather | solution.py:106
  78.6 3.2 %collective-permute-start = (s32[8,256]{1,0:T(8,128)S(1)}, s32[8,256]{1,0:T(8,128)S(1)}, u32[]{:S(2)}, u32[]{:S(2)}) collective-permute-start(s32[8,256]{1,0:T(8,128)S(1)} %bitcast.41), channel_id=1, source_target_pairs={{0,8},{1,9},{2,10},{3,11},{4,12},{5,13},{6,14},{7,15},{8,0},{9,1},... | collective-permute-start | bytes 24584 | tf_op jit(solution)/shard_map/ppermute | solution.py:110
  81.8 32.6 %collective-permute-done = s32[8,256]{1,0:T(8,128)S(1)} collective-permute-done((s32[8,256]{1,0:T(8,128)S(1)}, s32[8,256]{1,0:T(8,128)S(1)}, u32[]{:S(2)}, u32[]{:S(2)}) %collective-permute-start) | collective-permute-done | bytes 8224 | tf_op jit(solution)/shard_map/ppermute | solution.py:110
  114.4 2.0 %collective-permute-start.1 = (s32[16,256]{1,0:T(8,128)S(1)}, s32[16,256]{1,0:T(8,128)S(1)}, u32[]{:S(2)}, u32[]{:S(2)}) collective-permute-start(s32[16,256]{1,0:T(8,128)S(1)} %pad_add_fusion.2), channel_id=1, source_target_pairs={{0,16},{1,17},{2,18},{3,19},{4,20},{5,21},{6,22},{7,23},{8,24},{9,... | collective-permute-start | bytes 49160 | tf_op jit(solution)/shard_map/ppermute | solution.py:110
  116.4 3.5 %collective-permute-done.1 = s32[16,256]{1,0:T(8,128)S(1)} collective-permute-done((s32[16,256]{1,0:T(8,128)S(1)}, s32[16,256]{1,0:T(8,128)S(1)}, u32[]{:S(2)}, u32[]{:S(2)}) %collective-permute-start.1) | collective-permute-done | bytes 16416 | tf_op jit(solution)/shard_map/ppermute | solution.py:110
  119.9 0.1 copy.22
  120.0 6.7 %collective-permute-start.2 = (s32[32,256]{0,1:T(8,128)S(1)}, s32[32,256]{0,1:T(8,128)S(1)}, u32[]{:S(2)}, u32[]{:S(2)}) collective-permute-start(s32[32,256]{0,1:T(8,128)S(1)} %copy.22), channel_id=1, source_target_pairs={{0,32},{1,33},{2,34},{3,35},{4,36},{5,37},{6,38},{7,39},{8,40},{9,... | collective-permute-start | bytes 98312 | tf_op jit(solution)/shard_map/ppermute | solution.py:110
  126.8 2.8 %collective-permute-done.2 = s32[32,256]{0,1:T(8,128)S(1)} collective-permute-done((s32[32,256]{0,1:T(8,128)S(1)}, s32[32,256]{0,1:T(8,128)S(1)}, u32[]{:S(2)}, u32[]{:S(2)}) %collective-permute-start.2) | collective-permute-done | bytes 32800 | tf_op jit(solution)/shard_map/ppermute | solution.py:110
  129.7 0.1 pad_add_fusion
  129.8 0.1 copy.26
  129.9 0.1 copy.27
  130.0 24.7 %all_gather.8 = s32[16,16,256]{2,1,0:T(8,128)S(1)} all-gather(s32[1,16,256]{2,1,0:T(8,128)S(1)} %copy.27), channel_id=1, replica_groups=mesh['grp'=16,'ep'=64] {'grp'}, dimensions={0}, use_global_device_ids=true | all-gather | bytes 278528 | tf_op jit(solution)/shard_map/all_gather | solution.py:138
  154.8 0.1 copy.28
  154.9 0.4 copy.29
  155.3 0.3 eq.32
  155.6 1.4 fusion.2
  157.0 16.8 %all_to_all.39 = bf16[16,32,256]{2,1,0:T(8,128)(2,1)S(1)} all-to-all(bf16[16,32,256]{2,1,0:T(8,128)(2,1)S(1)} %bitcast.38), channel_id=1, replica_groups=mesh['grp'=16,'ep'=64] {'grp'}, dimensions={0} | all-to-all | bytes 524288 | tf_op jit(solution)/shard_map/all_to_all | solution.py:12
  173.8 25.3 %all_to_all.40 = bf16[16,32,256]{2,1,0:T(8,128)(2,1)S(1)} all-to-all(bf16[16,32,256]{2,1,0:T(8,128)(2,1)S(1)} %all_to_all.39), channel_id=1, replica_groups={{0,1,2,3,4,5,6,7,8,9,10,11,12,13,14,15},{16,17,18,19,20,21,22,23,24,25,..., dimensions={0} | all-to-all | bytes 524288 | tf_op jit(solution)/shard_map/all_to_all | solution.py:12
  199.1 0.7 copy.32
  (14 shorter events, 0.1 us)
Async XLA Ops:
  50.5 17.2 %copy-start = (s32[1,1,256]{2,1,0:T(1,128)S(1)}, s32[1,1,256]{2,1,0:T(1,128)}, u32[]{:S(2)}) copy-start(s32[1,1,256]{2,1,0:T(1,128)} %param.10) | copy-start | bytes 3076
  50.5 17.2 %copy-start.1 = (s32[1,1,256]{2,1,0:T(1,128)S(1)}, s32[1,1,256]{2,1,0:T(1,128)}, u32[]{:S(2)}) copy-start(s32[1,1,256]{2,1,0:T(1,128)} %param.9) | copy-start | bytes 3076
  50.5 105.1 %all-to-all-start.1 = ((bf16[64,64,256]{2,1,0:T(8,128)(2,1)}), bf16[64,64,256]{2,1,0:T(8,128)(2,1)S(1)}, u32[]{:S(2)}, u32[]{:S(2)}) async-start(bf16[64,64,256]{2,1,0:T(8,128)(2,1)} %bitcast.12), calls=%async_computation.1 | async-start | bytes 4194304 | tf_op jit(solution)/shard_map/all_to_all | solution.py:12
  78.6 35.7 %collective-permute-start = (s32[8,256]{1,0:T(8,128)S(1)}, s32[8,256]{1,0:T(8,128)S(1)}, u32[]{:S(2)}, u32[]{:S(2)}) collective-permute-start(s32[8,256]{1,0:T(8,128)S(1)} %bitcast.41), channel_id=1, source_target_pairs={{0,8},{1,9},{2,10},{3,11},{4,12},{5,13},{6,14},{7,15},{8,0},{9,1},... | collective-permute-start | bytes 24584 | tf_op jit(solution)/shard_map/ppermute | solution.py:110
  114.4 5.5 %collective-permute-start.1 = (s32[16,256]{1,0:T(8,128)S(1)}, s32[16,256]{1,0:T(8,128)S(1)}, u32[]{:S(2)}, u32[]{:S(2)}) collective-permute-start(s32[16,256]{1,0:T(8,128)S(1)} %pad_add_fusion.2), channel_id=1, source_target_pairs={{0,16},{1,17},{2,18},{3,19},{4,20},{5,21},{6,22},{7,23},{8,24},{9,... | collective-permute-start | bytes 49160 | tf_op jit(solution)/shard_map/ppermute | solution.py:110
  120.0 9.6 %collective-permute-start.2 = (s32[32,256]{0,1:T(8,128)S(1)}, s32[32,256]{0,1:T(8,128)S(1)}, u32[]{:S(2)}, u32[]{:S(2)}) collective-permute-start(s32[32,256]{0,1:T(8,128)S(1)} %copy.22), channel_id=1, source_target_pairs={{0,32},{1,33},{2,34},{3,35},{4,36},{5,37},{6,38},{7,39},{8,40},{9,... | collective-permute-start | bytes 98312 | tf_op jit(solution)/shard_map/ppermute | solution.py:110

commit v4 on v3

--- a/solution.py
+++ b/solution.py
@@ -99,19 +99,22 @@
     )(rows, weight)
 
 
-def gathered(index):
+def gathered(index, pick):
     columns = lax.axis_size("ep")
     near = min(8, columns // 2)
-    groups = [[i * near + j for j in range(near)] for i in range(columns // near)]
-    index = lax.all_gather(index, "ep", axis=0, axis_index_groups=groups)
-    step = near
-    while step < columns:
+    index, step, bits = index[None], columns // 2, 0
+    while step >= near:
         upper = (lax.axis_index("ep") // step) % 2 == 1
         other = lax.ppermute(index, "ep", [(i, i ^ step) for i in range(columns)])
         low, high = jnp.where(upper, other, index), jnp.where(upper, index, other)
         index = jnp.concatenate([low, high], axis=0)
-        step *= 2
-    return index
+        step, bits = step // 2, bits + 1
+    index = pick(index)
+    groups = [[i * near + j for j in range(near)] for i in range(columns // near)]
+    index = lax.all_gather(index, "ep", axis=0, axis_index_groups=groups)
+    index = index.reshape((near,) + (2,) * bits + index.shape[2:])
+    order = tuple(range(bits, 0, -1)) + (0,) + tuple(range(bits + 1, index.ndim))
+    return index.transpose(order).reshape((columns,) + index.shape[bits + 1 :])
 
 
 def body(hidden, down_weight, slot_gate, slot_owner, slot_row, block_count):
@@ -122,14 +125,16 @@
     mates = columns // planes
     send = slot_total // columns
     strip = width // planes
-    tokens = planes * TOK_DEV
 
     rows = scaled_rows(hidden[0, 0], slot_gate[0], block_count[0], planes, mates, send)
     rows = exchange(rows, "grp")
 
+    def own_mate(value):
+        value = value.reshape(value.shape[0], mates, planes * send)
+        return lax.dynamic_index_in_dim(value, lax.axis_index("ep") // planes, axis=1, keepdims=False)
+
     index = slot_owner[0, 0] * TOK_DEV + slot_row[0, 0]
-    index = gathered(index).reshape(columns, mates, planes, send)
-    index = lax.dynamic_index_in_dim(index, lax.axis_index("ep") // planes, axis=1, keepdims=False)
+    index = gathered(index, own_mate).reshape(columns, planes, send)
     index = index.swapaxes(0, 1).reshape(planes, columns * send)
 
     product = strip_product(rows, down_weight[0], planes, mates, send)
@@ -139,14 +144,23 @@
     index = lax.dynamic_index_in_dim(index, lax.axis_index("grp"), axis=1, keepdims=False)
     index = index.reshape(planes, columns, send).swapaxes(0, 1).reshape(-1)
 
-    wanted = jnp.arange(tokens)
+    siblings = [[mate * planes + d for d in range(planes)] for mate in range(mates)]
+    shift = [b // 2 + planes // 2 * (b % 2) for b in range(planes)]
+    block = jnp.arange(planes)
+    owner = (lax.axis_index("grp") + block // 2 + planes // 2 * (block % 2)) % planes
+    wanted = (owner[:, None] * TOK_DEV + jnp.arange(TOK_DEV)[None, :]).reshape(-1)
     table = (wanted[:, None] == index[None, :]).astype(jnp.bfloat16)
     summed = jnp.dot(table, arrived, preferred_element_type=jnp.float32).astype(jnp.bfloat16)
 
-    summed = exchange(summed, "grp")
-    siblings = [[mate * planes + d for d in range(planes)] for mate in range(mates)]
     summed = exchange(summed, "ep", siblings)
-    return summed.reshape(planes, TOK_DEV, strip).swapaxes(0, 1).reshape(TOK_DEV, width)
+    summed = summed.reshape(planes, TOK_DEV, strip).swapaxes(0, 1).reshape(TOK_DEV, width)
+    route = [
+        (z * columns + mate * planes + b, (z + shift[b]) % planes * columns + mate * planes + z)
+        for z in range(planes)
+        for mate in range(mates)
+        for b in range(planes)
+    ]
+    return lax.ppermute(summed, ("grp", "ep"), route)
 
 
 def solution(mesh):

time: 200 us -> 219 us (1.095)
  the two profiles are of different devices: /device:TPU:1 before, /device:TPU:72 now
where the time goes in v4:
time: 219 us; the launch traced here: 218 us
  blocking collectives  101 us (46%)
  waiting for transfers between devices  79.6 us (36%)
  starting transfers between devices  25.5 us (12%)
  Pallas kernels  8.08 us (4%)
  local copies, waits for them, and re-layouts  2.44 us (1%)
    all_to_all x2, blocking collectives, exchange(): lax.all_to_all(value, axis, split_axis=0, concat_axis=0, tiled=True, axis...  58.6 us
    ppermute x3, waiting for transfers between devices, gathered(): other = lax.ppermute(index, 'ep', [(i, i ^ step) for i in range(columns)])  50.3 us
    all_gather x1, blocking collectives, body(): index = lax.all_gather(index, 'grp', axis=0)  29.4 us
    ppermute x1, waiting for transfers between devices, body(): return lax.ppermute(summed, ('grp', 'ep'), route)  29.3 us
    all_gather x1, blocking collectives, gathered(): index = lax.all_gather(index, 'ep', axis=0, axis_index_groups=groups)  13.2 us
    ppermute x3, starting transfers between devices, gathered(): other = lax.ppermute(index, 'ep', [(i, i ^ step) for i in range(columns)])  11.8 us
    all_to_all x1, starting transfers between devices, exchange(): lax.all_to_all(value, axis, split_axis=0, concat_axis=0, tiled=True, axis...  10.6 us
    pallas_call x1, Pallas kernels, strip_product(): pl.pallas_call(lambda *refs: product_kernel(planes, mates, send, *refs),...  5.76 us
  transfers between devices with their start and end apart: 5, of which 4 were waited for; matrix products, arithmetic and copies ran while one was open for 1% of the time, Pallas kernels for 0%

profile of v4, /device:TPU:72, one launch (start us, length us, event | category | flops | bytes accessed | tf_op | source)
XLA Modules:
  0.0 218.4 jit_solution(9253439232892572553)
XLA Ops:
  0.0 2.3 %scaled_rows.1 = bf16[256,1024]{1,0:T(8,128)(2,1)} custom-call(f32[1,256]{1,0:T(1,128)} %bitcast.37, s32[1,64]{1,0:T(1,128)} %bitcast.38, bf16[256,1024]{1,0:T(8,128)(2,1)} %bitcast.32), custom_call_target="tpu_custom_call" | custom-call | flops 524288 | bytes 1048576 | tf_op jit(solution)/shard_map/scaled_rows/pallas_call | solution.py:36
  2.3 46.9 %all_to_all.32 = bf16[16,16,1024]{2,1,0:T(8,128)(2,1)S(1)} all-to-all(bf16[16,16,1024]{2,1,0:T(8,128)(2,1)} %bitcast.28), channel_id=1, replica_groups=mesh['grp'=16,'ep'=64] {'grp'}, dimensions={0} | all-to-all | bytes 1048576 | tf_op jit(solution)/shard_map/all_to_all | solution.py:12
  49.3 5.8 %strip_product.1 = bf16[4,16,64,256]{3,2,1,0:T(8,128)(2,1)} custom-call(bf16[256,1024]{1,0:T(8,128)(2,1)S(1)} %bitcast.25, bf16[1024,4096]{1,0:T(8,128)(2,1)} %bitcast.26), custom_call_target="tpu_custom_call" | custom-call | flops 2147483648 | bytes 10485760 | tf_op jit(solution)/shard_map/strip_product/pallas_call | solution.py:83
  55.0 10.6 %all-to-all-start.1 = ((bf16[64,64,256]{2,1,0:T(8,128)(2,1)}), bf16[64,64,256]{2,1,0:T(8,128)(2,1)S(1)}, u32[]{:S(2)}, u32[]{:S(2)}) async-start(bf16[64,64,256]{2,1,0:T(8,128)(2,1)} %bitcast.13), calls=%async_computation.1 | async-start | bytes 4194304 | tf_op jit(solution)/shard_map/all_to_all | solution.py:12
  65.7 6.5 %collective-permute-start = (s32[1,256]{1,0:T(1,128)S(1)}, s32[1,256]{1,0:T(1,128)S(1)}, u32[]{:S(2)}, u32[]{:S(2)}) collective-permute-start(s32[1,256]{1,0:T(1,128)S(1)} %add_bitcast_fusion), channel_id=1, source_target_pairs={{0,32},{1,33},{2,34},{3,35},{4,36},{5,37},{6,38},{7,39},{8,40},{9,... | collective-permute-start | bytes 3080 | tf_op jit(solution)/shard_map/ppermute | solution.py:108
  72.2 43.9 %collective-permute-done = s32[1,256]{1,0:T(1,128)S(1)} collective-permute-done((s32[1,256]{1,0:T(1,128)S(1)}, s32[1,256]{1,0:T(1,128)S(1)}, u32[]{:S(2)}, u32[]{:S(2)}) %collective-permute-start) | collective-permute-done | bytes 1056 | tf_op jit(solution)/shard_map/ppermute | solution.py:108
  116.1 1.9 collective-permute-start.1
  118.1 4.4 %collective-permute-done.1 = s32[2,256]{1,0:T(2,128)S(1)} collective-permute-done((s32[2,256]{1,0:T(2,128)S(1)}, s32[2,256]{1,0:T(2,128)S(1)}, u32[]{:S(2)}, u32[]{:S(2)}) %collective-permute-start.1) | collective-permute-done | bytes 2080 | tf_op jit(solution)/shard_map/ppermute | solution.py:108
  122.5 3.3 %collective-permute-start.2 = (s32[4,256]{1,0:T(4,128)S(1)}, s32[4,256]{1,0:T(4,128)S(1)}, u32[]{:S(2)}, u32[]{:S(2)}) collective-permute-start(s32[4,256]{1,0:T(4,128)S(1)} %pad_add_fusion.1), channel_id=1, source_target_pairs={{0,8},{1,9},{2,10},{3,11},{4,12},{5,13},{6,14},{7,15},{8,0},{9,1},... | collective-permute-start | bytes 12296 | tf_op jit(solution)/shard_map/ppermute | solution.py:108
  125.9 0.1 add.102
  126.0 2.0 collective-permute-done.2
  128.1 13.2 %all-gather = s32[64,1,64]{2,1,0:T(1,128)S(1)} all-gather(s32[8,1,64]{2,1,0:T(1,128)S(1)} %constant_dynamic-slice_fusion.1), channel_id=2, replica_groups={{0,1,2,3,4,5,6,7},{8,9,10,11,12,13,14,15},{16,17,18,19,20,21,22,23},{24..., dimensions={0}, use_global_device_ids=true | all-gather | bytes 18432 | tf_op jit(solution)/shard_map/all_gather | solution.py:114
  141.4 0.2 copy.22
  141.6 0.3 reshape_reshape.3
  141.9 0.1 copy.23
  142.1 29.4 %all_gather.11 = s32[16,16,256]{2,1,0:T(8,128)S(1)} all-gather(s32[1,16,256]{2,1,0:T(8,128)S(1)} %copy.24), channel_id=1, replica_groups=mesh['grp'=16,'ep'=64] {'grp'}, dimensions={0}, use_global_device_ids=true | all-gather | bytes 278528 | tf_op jit(solution)/shard_map/all_gather | solution.py:143
  171.4 0.1 copy.25
  171.6 0.4 copy.26
  172.0 0.3 eq.35
  172.3 1.3 fusion.4
  173.6 11.7 %all_to_all.33 = bf16[16,32,256]{2,1,0:T(8,128)(2,1)S(1)} all-to-all(bf16[16,32,256]{2,1,0:T(8,128)(2,1)S(1)} %bitcast.34), channel_id=1, replica_groups={{0,1,2,3,4,5,6,7,8,9,10,11,12,13,14,15},{16,17,18,19,20,21,22,23,24,25,..., dimensions={0} | all-to-all | bytes 524288 | tf_op jit(solution)/shard_map/all_to_all | solution.py:12
  185.3 3.1 %collective-permute-start.3 = (bf16[32,4096]{1,0:T(8,128)(2,1)S(1)}, bf16[32,4096]{1,0:T(8,128)(2,1)S(1)}, u32[]{:S(2)}, u32[]{:S(2)}) collective-permute-start(bf16[32,4096]{1,0:T(8,128)(2,1)S(1)} %bitcast.33), channel_id=1, source_target_pairs={{0,0},{1,512},{2,64},{3,576},{4,128},{5,640},{6,192},{7,704},{8,25... | collective-permute-start | bytes 786440 | tf_op jit(solution)/shard_map/ppermute | solution.py:163
  188.4 29.3 %collective-permute-done.3 = bf16[32,4096]{1,0:T(8,128)(2,1)S(1)} collective-permute-done((bf16[32,4096]{1,0:T(8,128)(2,1)S(1)}, bf16[32,4096]{1,0:T(8,128)(2,1)S(1)}, u32[]{:S(2)}, u32[]{:S(2)}) %collective-permute-start.3) | collective-permute-done | bytes 262176 | tf_op jit(solution)/shard_map/ppermute | solution.py:163
  217.7 0.7 copy.30
  (19 shorter events, 0.3 us)
Async XLA Ops:
  55.0 10.6 %copy-start = (s32[1,1,256]{2,1,0:T(1,128)S(1)}, s32[1,1,256]{2,1,0:T(1,128)}, u32[]{:S(2)}) copy-start(s32[1,1,256]{2,1,0:T(1,128)} %param.10) | copy-start | bytes 3076
  55.0 10.6 %copy-start.1 = (s32[1,1,256]{2,1,0:T(1,128)S(1)}, s32[1,1,256]{2,1,0:T(1,128)}, u32[]{:S(2)}) copy-start(s32[1,1,256]{2,1,0:T(1,128)} %param.9) | copy-start | bytes 3076
  55.0 117.2 %all-to-all-start.1 = ((bf16[64,64,256]{2,1,0:T(8,128)(2,1)}), bf16[64,64,256]{2,1,0:T(8,128)(2,1)S(1)}, u32[]{:S(2)}, u32[]{:S(2)}) async-start(bf16[64,64,256]{2,1,0:T(8,128)(2,1)} %bitcast.13), calls=%async_computation.1 | async-start | bytes 4194304 | tf_op jit(solution)/shard_map/all_to_all | solution.py:12
  65.7 50.4 %collective-permute-start = (s32[1,256]{1,0:T(1,128)S(1)}, s32[1,256]{1,0:T(1,128)S(1)}, u32[]{:S(2)}, u32[]{:S(2)}) collective-permute-start(s32[1,256]{1,0:T(1,128)S(1)} %add_bitcast_fusion), channel_id=1, source_target_pairs={{0,32},{1,33},{2,34},{3,35},{4,36},{5,37},{6,38},{7,39},{8,40},{9,... | collective-permute-start | bytes 3080 | tf_op jit(solution)/shard_map/ppermute | solution.py:108
  116.1 6.4 %collective-permute-start.1 = (s32[2,256]{1,0:T(2,128)S(1)}, s32[2,256]{1,0:T(2,128)S(1)}, u32[]{:S(2)}, u32[]{:S(2)}) collective-permute-start(s32[2,256]{1,0:T(2,128)S(1)} %pad_add_fusion.2), channel_id=1, source_target_pairs={{0,16},{1,17},{2,18},{3,19},{4,20},{5,21},{6,22},{7,23},{8,24},{9,... | collective-permute-start | bytes 6152 | tf_op jit(solution)/shard_map/ppermute | solution.py:108
  122.5 5.5 %collective-permute-start.2 = (s32[4,256]{1,0:T(4,128)S(1)}, s32[4,256]{1,0:T(4,128)S(1)}, u32[]{:S(2)}, u32[]{:S(2)}) collective-permute-start(s32[4,256]{1,0:T(4,128)S(1)} %pad_add_fusion.1), channel_id=1, source_target_pairs={{0,8},{1,9},{2,10},{3,11},{4,12},{5,13},{6,14},{7,15},{8,0},{9,1},... | collective-permute-start | bytes 12296 | tf_op jit(solution)/shard_map/ppermute | solution.py:108
  185.3 32.4 %collective-permute-start.3 = (bf16[32,4096]{1,0:T(8,128)(2,1)S(1)}, bf16[32,4096]{1,0:T(8,128)(2,1)S(1)}, u32[]{:S(2)}, u32[]{:S(2)}) collective-permute-start(bf16[32,4096]{1,0:T(8,128)(2,1)S(1)} %bitcast.33), channel_id=1, source_target_pairs={{0,0},{1,512},{2,64},{3,576},{4,128},{5,640},{6,192},{7,704},{8,25... | collective-permute-start | bytes 786440 | tf_op jit(solution)/shard_map/ppermute | solution.py:163

commit v5 on v4

--- a/solution.py
+++ b/solution.py
@@ -18,24 +18,33 @@
     return jnp.dot(pick, rows, preferred_element_type=jnp.float32).astype(jnp.bfloat16)
 
 
-def scale_kernel(planes, mates, send, gate_ref, count_ref, hidden_ref, out_ref):
-    slots, columns = hidden_ref.shape[0], count_ref.shape[1]
+def scale_kernel(planes, mates, send, gate_ref, count_ref, hidden_ref, out_ref, rows, sem):
+    load = pltpu.make_async_copy(hidden_ref, rows, sem)
+    load.start()
+    slots, columns = rows.shape[0], count_ref.shape[1]
     slot = lax.broadcasted_iota(jnp.int32, (slots, 1), 0)
     own = slot == lax.broadcasted_iota(jnp.int32, (slots, slots), 1)
     gate = jnp.sum(jnp.where(own, gate_ref[...], 0.0), axis=1, keepdims=True)
     block = slot // send == lax.broadcasted_iota(jnp.int32, (slots, columns), 1)
     limit = jnp.sum(jnp.where(block, count_ref[...], 0).astype(jnp.float32), axis=1, keepdims=True)
     scale = jnp.where((slot % send).astype(jnp.float32) < limit, gate, 0.0)
-    scaled = (hidden_ref[...].astype(jnp.float32) * scale).astype(jnp.bfloat16)
-    place = lax.broadcasted_iota(jnp.int32, (slots, slots), 0)
-    plane, mate, slot = place // (mates * send), (place // send) % mates, place % send
-    out_ref[...] = moved(scaled, (mate * planes + plane) * send + slot)
+    plane, mate, slot = slot // (mates * send), (slot // send) % mates, slot % send
+    source = jnp.broadcast_to((mate * planes + plane) * send + slot, (slots, slots))
+    load.wait()
+    scaled = (rows[...].astype(jnp.float32) * scale).astype(jnp.bfloat16)
+    out_ref[...] = moved(scaled, source)
 
 
 def scaled_rows(hidden, gate, count, planes, mates, send):
     return pl.pallas_call(
         lambda *refs: scale_kernel(planes, mates, send, *refs),
         out_shape=jax.ShapeDtypeStruct(hidden.shape, jnp.bfloat16),
+        in_specs=[
+            pl.BlockSpec(memory_space=pltpu.VMEM),
+            pl.BlockSpec(memory_space=pltpu.VMEM),
+            pl.BlockSpec(memory_space=pltpu.HBM),
+        ],
+        scratch_shapes=[pltpu.VMEM(hidden.shape, hidden.dtype), pltpu.SemaphoreType.DMA],
         cost_estimate=pl.CostEstimate(flops=2 * hidden.size, bytes_accessed=4 * hidden.size, transcendentals=0),
         name="scaled_rows",
     )(gate, count, hidden)
@@ -56,9 +65,10 @@
     ]
     for load in loads:
         load.start()
-    place = lax.broadcasted_iota(jnp.int32, (count, count), 0)
+    place = lax.broadcasted_iota(jnp.int32, (count, 1), 0)
     mate, group, slot = place // (planes * send), (place // send) % planes, place % send
-    rows = moved(rows_ref[...], (group * mates + mate) * send + slot)
+    source = jnp.broadcast_to((group * mates + mate) * send + slot, (count, count))
+    rows = moved(rows_ref[...], source)
     bundle = planes * send
     for i in range(pieces):
         loads[i].wait()
@@ -144,23 +154,14 @@
     index = lax.dynamic_index_in_dim(index, lax.axis_index("grp"), axis=1, keepdims=False)
     index = index.reshape(planes, columns, send).swapaxes(0, 1).reshape(-1)
 
-    siblings = [[mate * planes + d for d in range(planes)] for mate in range(mates)]
-    shift = [b // 2 + planes // 2 * (b % 2) for b in range(planes)]
-    block = jnp.arange(planes)
-    owner = (lax.axis_index("grp") + block // 2 + planes // 2 * (block % 2)) % planes
-    wanted = (owner[:, None] * TOK_DEV + jnp.arange(TOK_DEV)[None, :]).reshape(-1)
+    wanted = jnp.arange(planes * TOK_DEV)
     table = (wanted[:, None] == index[None, :]).astype(jnp.bfloat16)
     summed = jnp.dot(table, arrived, preferred_element_type=jnp.float32).astype(jnp.bfloat16)
 
+    summed = exchange(summed, "grp")
+    siblings = [[mate * planes + d for d in range(planes)] for mate in range(mates)]
     summed = exchange(summed, "ep", siblings)
-    summed = summed.reshape(planes, TOK_DEV, strip).swapaxes(0, 1).reshape(TOK_DEV, width)
-    route = [
-        (z * columns + mate * planes + b, (z + shift[b]) % planes * columns + mate * planes + z)
-        for z in range(planes)
-        for mate in range(mates)
-        for b in range(planes)
-    ]
-    return lax.ppermute(summed, ("grp", "ep"), route)
+    return summed.reshape(planes, TOK_DEV, strip).swapaxes(0, 1).reshape(TOK_DEV, width)
 
 
 def solution(mesh):

time: 219 us -> 210 us (0.959)
  the two profiles are of different devices: /device:TPU:72 before, /device:TPU:1 now
where the time goes in v5:
time: 210 us
  blocking collectives  121 us (58%)
  waiting for transfers between devices  46 us (22%)
  starting transfers between devices  30.7 us (15%)
  Pallas kernels  8.59 us (4%)
  local copies, waits for them, and re-layouts  2.36 us (1%)
    all_to_all x3, blocking collectives, exchange(): lax.all_to_all(value, axis, split_axis=0, concat_axis=0, tiled=True, axis...  78.5 us
    ppermute x3, waiting for transfers between devices, gathered(): other = lax.ppermute(index, 'ep', [(i, i ^ step) for i in range(columns)])  46 us
    all_gather x1, blocking collectives, body(): index = lax.all_gather(index, 'grp', axis=0)  25 us
    all_to_all x1, starting transfers between devices, exchange(): lax.all_to_all(value, axis, split_axis=0, concat_axis=0, tiled=True, axis...  17.1 us
    all_gather x1, blocking collectives, gathered(): index = lax.all_gather(index, 'ep', axis=0, axis_index_groups=groups)  17.1 us
    ppermute x3, starting transfers between devices, gathered(): other = lax.ppermute(index, 'ep', [(i, i ^ step) for i in range(columns)])  13.5 us
    pallas_call x1, Pallas kernels, strip_product(): pl.pallas_call(lambda *refs: product_kernel(planes, mates, send, *refs),...  5.74 us
  transfers between devices with their start and end apart: 4, of which 3 were waited for; matrix products, arithmetic and copies ran while one was open for 1% of the time, Pallas kernels for 0%

profile of v5, /device:TPU:1, one launch (start us, length us, event | category | flops | bytes accessed | tf_op | source)
XLA Modules:
  0.0 209.9 jit_solution(15867706158524358046)
XLA Ops:
  0.0 2.9 %scaled_rows.1 = bf16[256,1024]{1,0:T(8,128)(2,1)} custom-call(f32[1,256]{1,0:T(1,128)} %bitcast.36, s32[1,64]{1,0:T(1,128)} %bitcast.37, bf16[256,1024]{1,0:T(8,128)(2,1)} %bitcast.32), custom_call_target="tpu_custom_call" | custom-call | flops 524288 | bytes 1048576 | tf_op jit(solution)/shard_map/scaled_rows/pallas_call | solution.py:39
  2.9 42.4 %all_to_all.38 = bf16[16,16,1024]{2,1,0:T(8,128)(2,1)S(1)} all-to-all(bf16[16,16,1024]{2,1,0:T(8,128)(2,1)} %bitcast.28), channel_id=1, replica_groups=mesh['grp'=16,'ep'=64] {'grp'}, dimensions={0} | all-to-all | bytes 1048576 | tf_op jit(solution)/shard_map/all_to_all | solution.py:12
  45.3 5.7 %strip_product.1 = bf16[4,16,64,256]{3,2,1,0:T(8,128)(2,1)} custom-call(bf16[256,1024]{1,0:T(8,128)(2,1)S(1)} %bitcast.25, bf16[1024,4096]{1,0:T(8,128)(2,1)} %bitcast.26), custom_call_target="tpu_custom_call" | custom-call | flops 2147483648 | bytes 10485760 | tf_op jit(solution)/shard_map/strip_product/pallas_call | solution.py:93
  51.1 17.1 %all-to-all-start.1 = ((bf16[64,64,256]{2,1,0:T(8,128)(2,1)}), bf16[64,64,256]{2,1,0:T(8,128)(2,1)S(1)}, u32[]{:S(2)}, u32[]{:S(2)}) async-start(bf16[64,64,256]{2,1,0:T(8,128)(2,1)} %bitcast.13), calls=%async_computation.1 | async-start | bytes 4194304 | tf_op jit(solution)/shard_map/all_to_all | solution.py:12
  68.2 7.3 %collective-permute-start = (s32[1,256]{1,0:T(1,128)S(1)}, s32[1,256]{1,0:T(1,128)S(1)}, u32[]{:S(2)}, u32[]{:S(2)}) collective-permute-start(s32[1,256]{1,0:T(1,128)S(1)} %add_bitcast_fusion), channel_id=1, source_target_pairs={{0,32},{1,33},{2,34},{3,35},{4,36},{5,37},{6,38},{7,39},{8,40},{9,... | collective-permute-start | bytes 3080 | tf_op jit(solution)/shard_map/ppermute | solution.py:118
  75.5 42.2 %collective-permute-done = s32[1,256]{1,0:T(1,128)S(1)} collective-permute-done((s32[1,256]{1,0:T(1,128)S(1)}, s32[1,256]{1,0:T(1,128)S(1)}, u32[]{:S(2)}, u32[]{:S(2)}) %collective-permute-start) | collective-permute-done | bytes 1056 | tf_op jit(solution)/shard_map/ppermute | solution.py:118
  117.8 2.3 %collective-permute-start.1 = (s32[2,256]{1,0:T(2,128)S(1)}, s32[2,256]{1,0:T(2,128)S(1)}, u32[]{:S(2)}, u32[]{:S(2)}) collective-permute-start(s32[2,256]{1,0:T(2,128)S(1)} %pad_add_fusion.2), channel_id=1, source_target_pairs={{0,16},{1,17},{2,18},{3,19},{4,20},{5,21},{6,22},{7,23},{8,24},{9,... | collective-permute-start | bytes 6152 | tf_op jit(solution)/shard_map/ppermute | solution.py:118
  120.1 2.9 %collective-permute-done.1 = s32[2,256]{1,0:T(2,128)S(1)} collective-permute-done((s32[2,256]{1,0:T(2,128)S(1)}, s32[2,256]{1,0:T(2,128)S(1)}, u32[]{:S(2)}, u32[]{:S(2)}) %collective-permute-start.1) | collective-permute-done | bytes 2080 | tf_op jit(solution)/shard_map/ppermute | solution.py:118
  123.0 3.9 %collective-permute-start.2 = (s32[4,256]{1,0:T(4,128)S(1)}, s32[4,256]{1,0:T(4,128)S(1)}, u32[]{:S(2)}, u32[]{:S(2)}) collective-permute-start(s32[4,256]{1,0:T(4,128)S(1)} %pad_add_fusion.1), channel_id=1, source_target_pairs={{0,8},{1,9},{2,10},{3,11},{4,12},{5,13},{6,14},{7,15},{8,0},{9,1},... | collective-permute-start | bytes 12296 | tf_op jit(solution)/shard_map/ppermute | solution.py:118
  127.0 0.9 collective-permute-done.2
  128.0 0.1 reshape.51
  128.1 17.1 %all-gather = s32[64,1,64]{2,1,0:T(1,128)S(1)} all-gather(s32[8,1,64]{2,1,0:T(1,128)S(1)} %constant_dynamic-slice_fusion.1), channel_id=2, replica_groups={{0,1,2,3,4,5,6,7},{8,9,10,11,12,13,14,15},{16,17,18,19,20,21,22,23},{24..., dimensions={0}, use_global_device_ids=true | all-gather | bytes 18432 | tf_op jit(solution)/shard_map/all_gather | solution.py:124
  145.2 0.2 copy.22
  145.4 0.3 reshape_reshape.3
  145.7 0.1 copy.23
  145.8 0.1 copy.24
  145.9 25.0 %all_gather.11 = s32[16,16,256]{2,1,0:T(8,128)S(1)} all-gather(s32[1,16,256]{2,1,0:T(8,128)S(1)} %copy.24), channel_id=1, replica_groups=mesh['grp'=16,'ep'=64] {'grp'}, dimensions={0}, use_global_device_ids=true | all-gather | bytes 278528 | tf_op jit(solution)/shard_map/all_gather | solution.py:153
  170.9 0.1 copy.25
  171.0 0.4 copy.26
  171.4 0.3 eq.32
  171.7 1.4 fusion.2
  173.1 16.8 %all_to_all.39 = bf16[16,32,256]{2,1,0:T(8,128)(2,1)S(1)} all-to-all(bf16[16,32,256]{2,1,0:T(8,128)(2,1)S(1)} %bitcast.33), channel_id=1, replica_groups=mesh['grp'=16,'ep'=64] {'grp'}, dimensions={0} | all-to-all | bytes 524288 | tf_op jit(solution)/shard_map/all_to_all | solution.py:12
  189.8 19.3 %all_to_all.40 = bf16[16,32,256]{2,1,0:T(8,128)(2,1)S(1)} all-to-all(bf16[16,32,256]{2,1,0:T(8,128)(2,1)S(1)} %all_to_all.39), channel_id=1, replica_groups={{0,1,2,3,4,5,6,7,8,9,10,11,12,13,14,15},{16,17,18,19,20,21,22,23,24,25,..., dimensions={0} | all-to-all | bytes 524288 | tf_op jit(solution)/shard_map/all_to_all | solution.py:12
  209.2 0.7 copy.28
  (14 shorter events, 0.1 us)
Async XLA Ops:
  51.0 17.2 %copy-start = (s32[1,1,256]{2,1,0:T(1,128)S(1)}, s32[1,1,256]{2,1,0:T(1,128)}, u32[]{:S(2)}) copy-start(s32[1,1,256]{2,1,0:T(1,128)} %param.10) | copy-start | bytes 3076
  51.0 17.2 %copy-start.1 = (s32[1,1,256]{2,1,0:T(1,128)S(1)}, s32[1,1,256]{2,1,0:T(1,128)}, u32[]{:S(2)}) copy-start(s32[1,1,256]{2,1,0:T(1,128)} %param.9) | copy-start | bytes 3076
  51.1 120.7 %all-to-all-start.1 = ((bf16[64,64,256]{2,1,0:T(8,128)(2,1)}), bf16[64,64,256]{2,1,0:T(8,128)(2,1)S(1)}, u32[]{:S(2)}, u32[]{:S(2)}) async-start(bf16[64,64,256]{2,1,0:T(8,128)(2,1)} %bitcast.13), calls=%async_computation.1 | async-start | bytes 4194304 | tf_op jit(solution)/shard_map/all_to_all | solution.py:12
  68.2 49.5 %collective-permute-start = (s32[1,256]{1,0:T(1,128)S(1)}, s32[1,256]{1,0:T(1,128)S(1)}, u32[]{:S(2)}, u32[]{:S(2)}) collective-permute-start(s32[1,256]{1,0:T(1,128)S(1)} %add_bitcast_fusion), channel_id=1, source_target_pairs={{0,32},{1,33},{2,34},{3,35},{4,36},{5,37},{6,38},{7,39},{8,40},{9,... | collective-permute-start | bytes 3080 | tf_op jit(solution)/shard_map/ppermute | solution.py:118
  117.8 5.2 %collective-permute-start.1 = (s32[2,256]{1,0:T(2,128)S(1)}, s32[2,256]{1,0:T(2,128)S(1)}, u32[]{:S(2)}, u32[]{:S(2)}) collective-permute-start(s32[2,256]{1,0:T(2,128)S(1)} %pad_add_fusion.2), channel_id=1, source_target_pairs={{0,16},{1,17},{2,18},{3,19},{4,20},{5,21},{6,22},{7,23},{8,24},{9,... | collective-permute-start | bytes 6152 | tf_op jit(solution)/shard_map/ppermute | solution.py:118
  123.0 4.9 %collective-permute-start.2 = (s32[4,256]{1,0:T(4,128)S(1)}, s32[4,256]{1,0:T(4,128)S(1)}, u32[]{:S(2)}, u32[]{:S(2)}) collective-permute-start(s32[4,256]{1,0:T(4,128)S(1)} %pad_add_fusion.1), channel_id=1, source_target_pairs={{0,8},{1,9},{2,10},{3,11},{4,12},{5,13},{6,14},{7,15},{8,0},{9,1},... | collective-permute-start | bytes 12296 | tf_op jit(solution)/shard_map/ppermute | solution.py:118

commit v6 on v3

--- a/solution.py
+++ b/solution.py
@@ -26,10 +26,10 @@
     block = slot // send == lax.broadcasted_iota(jnp.int32, (slots, columns), 1)
     limit = jnp.sum(jnp.where(block, count_ref[...], 0).astype(jnp.float32), axis=1, keepdims=True)
     scale = jnp.where((slot % send).astype(jnp.float32) < limit, gate, 0.0)
+    plane, mate, slot = slot // (mates * send), (slot // send) % mates, slot % send
+    source = jnp.broadcast_to((mate * planes + plane) * send + slot, (slots, slots))
     scaled = (hidden_ref[...].astype(jnp.float32) * scale).astype(jnp.bfloat16)
-    place = lax.broadcasted_iota(jnp.int32, (slots, slots), 0)
-    plane, mate, slot = place // (mates * send), (place // send) % mates, place % send
-    out_ref[...] = moved(scaled, (mate * planes + plane) * send + slot)
+    out_ref[...] = moved(scaled, source)
 
 
 def scaled_rows(hidden, gate, count, planes, mates, send):
@@ -56,9 +56,10 @@
     ]
     for load in loads:
         load.start()
-    place = lax.broadcasted_iota(jnp.int32, (count, count), 0)
+    place = lax.broadcasted_iota(jnp.int32, (count, 1), 0)
     mate, group, slot = place // (planes * send), (place // send) % planes, place % send
-    rows = moved(rows_ref[...], (group * mates + mate) * send + slot)
+    source = jnp.broadcast_to((group * mates + mate) * send + slot, (count, count))
+    rows = moved(rows_ref[...], source)
     bundle = planes * send
     for i in range(pieces):
         loads[i].wait()
@@ -99,19 +100,16 @@
     )(rows, weight)
 
 
-def gathered(index):
+def doubled(index, near):
     columns = lax.axis_size("ep")
-    near = min(8, columns // 2)
-    groups = [[i * near + j for j in range(near)] for i in range(columns // near)]
-    index = lax.all_gather(index, "ep", axis=0, axis_index_groups=groups)
-    step = near
-    while step < columns:
+    step, bits = columns // 2, 0
+    while step >= near:
         upper = (lax.axis_index("ep") // step) % 2 == 1
         other = lax.ppermute(index, "ep", [(i, i ^ step) for i in range(columns)])
         low, high = jnp.where(upper, other, index), jnp.where(upper, index, other)
-        index = jnp.concatenate([low, high], axis=0)
-        step *= 2
-    return index
+        index = jnp.stack([low, high], axis=0)
+        step, bits = step // 2, bits + 1
+    return index, bits
 
 
 def body(hidden, down_weight, slot_gate, slot_owner, slot_row, block_count):
@@ -122,24 +120,30 @@
     mates = columns // planes
     send = slot_total // columns
     strip = width // planes
-    tokens = planes * TOK_DEV
 
     rows = scaled_rows(hidden[0, 0], slot_gate[0], block_count[0], planes, mates, send)
     rows = exchange(rows, "grp")
 
+    near = min(8, columns // 2)
     index = slot_owner[0, 0] * TOK_DEV + slot_row[0, 0]
-    index = gathered(index).reshape(columns, mates, planes, send)
+    index, bits = doubled(index, near)
+    index = index.reshape(columns // near, mates, planes, send)
     index = lax.dynamic_index_in_dim(index, lax.axis_index("ep") // planes, axis=1, keepdims=False)
-    index = index.swapaxes(0, 1).reshape(planes, columns * send)
+    index = index.swapaxes(0, 1).reshape(planes, columns // near * send)
 
+    rows, index = lax.optimization_barrier((rows, index))
     product = strip_product(rows, down_weight[0], planes, mates, send)
     arrived = exchange(product.reshape(columns * planes * send, strip), "ep")
 
     index = lax.all_gather(index, "grp", axis=0)
     index = lax.dynamic_index_in_dim(index, lax.axis_index("grp"), axis=1, keepdims=False)
-    index = index.reshape(planes, columns, send).swapaxes(0, 1).reshape(-1)
+    groups = [[i * near + j for j in range(near)] for i in range(columns // near)]
+    index = lax.all_gather(index, "ep", axis=0, axis_index_groups=groups)
+    index = index.reshape((near, planes) + (2,) * bits + (send,))
+    order = tuple(range(bits + 1, 1, -1)) + (0, 1, bits + 2)
+    index = index.transpose(order).reshape(-1)
 
-    wanted = jnp.arange(tokens)
+    wanted = jnp.arange(planes * TOK_DEV)
     table = (wanted[:, None] == index[None, :]).astype(jnp.bfloat16)
     summed = jnp.dot(table, arrived, preferred_element_type=jnp.float32).astype(jnp.bfloat16)
 

time: 200 us -> 158 us (0.79)
  blocking collectives: 120 us -> 82.3 us
  waiting for transfers between devices: 38.9 us -> 12 us
  starting transfers between devices: 29 us -> 51.1 us
    all_to_all x3 -> x2, blocking collectives: 84.5 us -> 37.7 us  [exchange(): lax.all_to_all(value, axis, split_axis=0, concat_axis=0, tiled=True, axis...]
    ppermute x3, waiting for transfers between devices: 38.9 us -> 4.22 us  [doubled(): other = lax.ppermute(index, 'ep', [(i, i ^ step) for i in range(columns)])]
    all_to_all x1 -> x2, starting transfers between devices: 17.1 us -> 36.6 us  [exchange(): lax.all_to_all(value, axis, split_axis=0, concat_axis=0, tiled=True, axis...]
    all_to_all x1 -> x2, waiting for transfers between devices: 0.01 us -> 7.82 us  [exchange(): lax.all_to_all(value, axis, split_axis=0, concat_axis=0, tiled=True, axis...]
    all_gather x1, blocking collectives: 10.9 us -> 18.4 us  [body(): index = lax.all_gather(index, 'ep', axis=0, axis_index_groups=groups)]
    ppermute x3, starting transfers between devices: 11.9 us -> 14.5 us  [doubled(): other = lax.ppermute(index, 'ep', [(i, i ^ step) for i in range(columns)])]
  transfers between devices with their start and end apart: 4 -> 5, of which waited for: 3 -> 5; matrix products, arithmetic and copies ran while one was open for 1% -> 1% of each run, Pallas kernels for 0% -> 0%
where the time goes in v6:
time: 158 us; the launch traced here: 157 us
  blocking collectives  82.3 us (52%)
  starting transfers between devices  51.1 us (32%)
  waiting for transfers between devices  12 us (8%)
  Pallas kernels  8.08 us (5%)
  local copies, waits for them, and re-layouts  2.08 us (1%)
    all_to_all x2, blocking collectives, exchange(): lax.all_to_all(value, axis, split_axis=0, concat_axis=0, tiled=True, axis...  37.7 us
    all_to_all x2, starting transfers between devices, exchange(): lax.all_to_all(value, axis, split_axis=0, concat_axis=0, tiled=True, axis...  36.6 us
    all_gather x1, blocking collectives, body(): index = lax.all_gather(index, 'grp', axis=0)  26.2 us
    all_gather x1, blocking collectives, body(): index = lax.all_gather(index, 'ep', axis=0, axis_index_groups=groups)  18.4 us
    ppermute x3, starting transfers between devices, doubled(): other = lax.ppermute(index, 'ep', [(i, i ^ step) for i in range(columns)])  14.5 us
    all_to_all x2, waiting for transfers between devices, exchange(): lax.all_to_all(value, axis, split_axis=0, concat_axis=0, tiled=True, axis...  7.82 us
    pallas_call x1, Pallas kernels, strip_product(): pl.pallas_call(lambda *refs: product_kernel(planes, mates, send, *refs),...  5.73 us
    ppermute x3, waiting for transfers between devices, doubled(): other = lax.ppermute(index, 'ep', [(i, i ^ step) for i in range(columns)])  4.22 us
  transfers between devices with their start and end apart: 5, of which 5 were waited for; matrix products, arithmetic and copies ran while one was open for 1% of the time, Pallas kernels for 0%

profile of v6, /device:TPU:1, one launch (start us, length us, event | category | flops | bytes accessed | tf_op | source)
XLA Modules:
  0.0 157.2 jit_solution(11315706876484161297)
XLA Ops:
  0.0 2.3 %scaled_rows.1 = bf16[256,1024]{1,0:T(8,128)(2,1)} custom-call(f32[1,256]{1,0:T(1,128)} %bitcast.51, s32[1,64]{1,0:T(1,128)} %bitcast.52, bf16[256,1024]{1,0:T(8,128)(2,1)} %bitcast.41), custom_call_target="tpu_custom_call" | custom-call | flops 524288 | bytes 1048576 | tf_op jit(solution)/shard_map/scaled_rows/pallas_call | solution.py:36
  2.4 19.4 %all-to-all-start = ((bf16[16,16,1024]{2,1,0:T(8,128)(2,1)}), bf16[16,16,1024]{2,1,0:T(8,128)(2,1)S(1)}, u32[]{:S(2)}, u32[]{:S(2)}) async-start(bf16[16,16,1024]{2,1,0:T(8,128)(2,1)} %bitcast.38), calls=%async_computation | async-start | bytes 1048576 | tf_op jit(solution)/shard_map/all_to_all | solution.py:12
  21.8 7.5 %collective-permute-start = (s32[256]{0:T(256)S(1)}, s32[256]{0:T(256)S(1)}, u32[]{:S(2)}, u32[]{:S(2)}) collective-permute-start(s32[256]{0:T(256)S(1)} %bitcast.49), channel_id=1, source_target_pairs={{0,32},{1,33},{2,34},{3,35},{4,36},{5,37},{6,38},{7,39},{8,40},{9,... | collective-permute-start | bytes 3080 | tf_op jit(solution)/shard_map/ppermute | solution.py:108
  29.3 1.2 collective-permute-done
  30.5 4.0 %collective-permute-start.1 = (s32[2,256]{1,0:T(2,128)S(1)}, s32[2,256]{1,0:T(2,128)S(1)}, u32[]{:S(2)}, u32[]{:S(2)}) collective-permute-start(s32[2,256]{1,0:T(2,128)S(1)} %pad_add_fusion.2), channel_id=1, source_target_pairs={{0,16},{1,17},{2,18},{3,19},{4,20},{5,21},{6,22},{7,23},{8,24},{9,... | collective-permute-start | bytes 6152 | tf_op jit(solution)/shard_map/ppermute | solution.py:108
  34.6 1.4 collective-permute-done.1
  36.1 3.0 %collective-permute-start.2 = (s32[2,2,256]{2,1,0:T(2,128)S(1)}, s32[2,2,256]{2,1,0:T(2,128)S(1)}, u32[]{:S(2)}, u32[]{:S(2)}) collective-permute-start(s32[2,2,256]{2,1,0:T(2,128)S(1)} %pad_add_fusion.1), channel_id=1, source_target_pairs={{0,8},{1,9},{2,10},{3,11},{4,12},{5,13},{6,14},{7,15},{8,0},{9,1},... | collective-permute-start | bytes 12296 | tf_op jit(solution)/shard_map/ppermute | solution.py:108
  39.1 1.6 collective-permute-done.2
  40.7 0.3 reshape.30
  41.0 0.1 copy.18
  41.1 3.6 %all-to-all-done = bf16[16,16,1024]{2,1,0:T(8,128)(2,1)S(1)} async-done(((bf16[16,16,1024]{2,1,0:T(8,128)(2,1)}), bf16[16,16,1024]{2,1,0:T(8,128)(2,1)S(1)}, u32[]{:S(2)}, u32[]{:S(2)}) %all-to-all-start) | async-done | bytes 524320 | tf_op jit(solution)/shard_map/all_to_all | solution.py:12
  44.8 5.7 %strip_product.1 = bf16[4,16,64,256]{3,2,1,0:T(8,128)(2,1)} custom-call(bf16[256,1024]{1,0:T(8,128)(2,1)S(1)} %bitcast.35, bf16[1024,4096]{1,0:T(8,128)(2,1)} %bitcast.36), custom_call_target="tpu_custom_call" | custom-call | flops 2147483648 | bytes 10485760 | tf_op jit(solution)/shard_map/strip_product/pallas_call | solution.py:84
  50.5 17.1 %all-to-all-start.1 = ((bf16[64,64,256]{2,1,0:T(8,128)(2,1)}), bf16[64,64,256]{2,1,0:T(8,128)(2,1)S(1)}, u32[]{:S(2)}, u32[]{:S(2)}) async-start(bf16[64,64,256]{2,1,0:T(8,128)(2,1)} %bitcast.19), calls=%async_computation.1 | async-start | bytes 4194304 | tf_op jit(solution)/shard_map/all_to_all | solution.py:12
  67.7 0.1 copy.19
  67.7 26.2 %all-gather = s32[256,32]{1,0:T(8,128)S(1)} all-gather(s32[16,32]{1,0:T(8,128)S(1)} %copy.19), channel_id=2, replica_groups=mesh['grp'=16,'ep'=64] {'grp'}, dimensions={0}, use_global_device_ids=true | all-gather | bytes 34816 | tf_op jit(solution)/shard_map/all_gather | solution.py:138
  93.9 18.4 %all-gather.1 = s32[128,1,32]{2,1,0:T(1,128)S(1)} all-gather(s32[16,1,32]{2,1,0:T(1,128)S(1)} %constant_dynamic-slice_fusion), channel_id=3, replica_groups={{0,1,2,3,4,5,6,7},{8,9,10,11,12,13,14,15},{16,17,18,19,20,21,22,23},{24..., dimensions={0}, use_global_device_ids=true | all-gather | bytes 18432 | tf_op jit(solution)/shard_map/all_gather | solution.py:141
  112.4 0.1 reshape.32
  112.5 0.4 copy.21
  112.9 0.3 eq.32
  113.2 4.2 %all-to-all-done.1 = bf16[64,64,256]{2,1,0:T(8,128)(2,1)S(1)} async-done(((bf16[64,64,256]{2,1,0:T(8,128)(2,1)}), bf16[64,64,256]{2,1,0:T(8,128)(2,1)S(1)}, u32[]{:S(2)}, u32[]{:S(2)}) %all-to-all-start.1) | async-done | bytes 2097184 | tf_op jit(solution)/shard_map/all_to_all | solution.py:12
  117.4 1.4 fusion.2
  118.7 18.6 %all_to_all.39 = bf16[16,32,256]{2,1,0:T(8,128)(2,1)S(1)} all-to-all(bf16[16,32,256]{2,1,0:T(8,128)(2,1)S(1)} %bitcast.42), channel_id=1, replica_groups=mesh['grp'=16,'ep'=64] {'grp'}, dimensions={0} | all-to-all | bytes 524288 | tf_op jit(solution)/shard_map/all_to_all | solution.py:12
  137.3 19.1 %all_to_all.40 = bf16[16,32,256]{2,1,0:T(8,128)(2,1)S(1)} all-to-all(bf16[16,32,256]{2,1,0:T(8,128)(2,1)S(1)} %all_to_all.39), channel_id=1, replica_groups={{0,1,2,3,4,5,6,7,8,9,10,11,12,13,14,15},{16,17,18,19,20,21,22,23,24,25,..., dimensions={0} | all-to-all | bytes 524288 | tf_op jit(solution)/shard_map/all_to_all | solution.py:12
  156.5 0.7 copy.24
  (14 shorter events, 0.1 us)
Async XLA Ops:
  0.0 21.8 %copy-start = (s32[1,1,256]{2,1,0:T(1,128)S(1)}, s32[1,1,256]{2,1,0:T(1,128)}, u32[]{:S(2)}) copy-start(s32[1,1,256]{2,1,0:T(1,128)} %param.10) | copy-start | bytes 3076
  0.0 21.8 %copy-start.1 = (s32[1,1,256]{2,1,0:T(1,128)S(1)}, s32[1,1,256]{2,1,0:T(1,128)}, u32[]{:S(2)}) copy-start(s32[1,1,256]{2,1,0:T(1,128)} %param.9) | copy-start | bytes 3076
  2.4 42.4 %all-to-all-start = ((bf16[16,16,1024]{2,1,0:T(8,128)(2,1)}), bf16[16,16,1024]{2,1,0:T(8,128)(2,1)S(1)}, u32[]{:S(2)}, u32[]{:S(2)}) async-start(bf16[16,16,1024]{2,1,0:T(8,128)(2,1)} %bitcast.38), calls=%async_computation | async-start | bytes 1048576 | tf_op jit(solution)/shard_map/all_to_all | solution.py:12
  21.8 8.7 %collective-permute-start = (s32[256]{0:T(256)S(1)}, s32[256]{0:T(256)S(1)}, u32[]{:S(2)}, u32[]{:S(2)}) collective-permute-start(s32[256]{0:T(256)S(1)} %bitcast.49), channel_id=1, source_target_pairs={{0,32},{1,33},{2,34},{3,35},{4,36},{5,37},{6,38},{7,39},{8,40},{9,... | collective-permute-start | bytes 3080 | tf_op jit(solution)/shard_map/ppermute | solution.py:108
  30.5 5.5 %collective-permute-start.1 = (s32[2,256]{1,0:T(2,128)S(1)}, s32[2,256]{1,0:T(2,128)S(1)}, u32[]{:S(2)}, u32[]{:S(2)}) collective-permute-start(s32[2,256]{1,0:T(2,128)S(1)} %pad_add_fusion.2), channel_id=1, source_target_pairs={{0,16},{1,17},{2,18},{3,19},{4,20},{5,21},{6,22},{7,23},{8,24},{9,... | collective-permute-start | bytes 6152 | tf_op jit(solution)/shard_map/ppermute | solution.py:108
  36.1 4.6 %collective-permute-start.2 = (s32[2,2,256]{2,1,0:T(2,128)S(1)}, s32[2,2,256]{2,1,0:T(2,128)S(1)}, u32[]{:S(2)}, u32[]{:S(2)}) collective-permute-start(s32[2,2,256]{2,1,0:T(2,128)S(1)} %pad_add_fusion.1), channel_id=1, source_target_pairs={{0,8},{1,9},{2,10},{3,11},{4,12},{5,13},{6,14},{7,15},{8,0},{9,1},... | collective-permute-start | bytes 12296 | tf_op jit(solution)/shard_map/ppermute | solution.py:108
  50.5 66.9 %all-to-all-start.1 = ((bf16[64,64,256]{2,1,0:T(8,128)(2,1)}), bf16[64,64,256]{2,1,0:T(8,128)(2,1)S(1)}, u32[]{:S(2)}, u32[]{:S(2)}) async-start(bf16[64,64,256]{2,1,0:T(8,128)(2,1)} %bitcast.19), calls=%async_computation.1 | async-start | bytes 4194304 | tf_op jit(solution)/shard_map/all_to_all | solution.py:12

commit v7 on v6

--- a/solution.py
+++ b/solution.py
@@ -6,6 +6,7 @@
 from jax.sharding import PartitionSpec as P
 
 TOK_DEV = 32
+STRIDE = 3
 
 
 def exchange(value, axis, groups=None):
@@ -26,7 +27,8 @@
     block = slot // send == lax.broadcasted_iota(jnp.int32, (slots, columns), 1)
     limit = jnp.sum(jnp.where(block, count_ref[...], 0).astype(jnp.float32), axis=1, keepdims=True)
     scale = jnp.where((slot % send).astype(jnp.float32) < limit, gate, 0.0)
-    plane, mate, slot = slot // (mates * send), (slot // send) % mates, slot % send
+    plane = slot // (mates * send) * pow(STRIDE, -1, planes) % planes
+    mate, slot = (slot // send) % mates, slot % send
     source = jnp.broadcast_to((mate * planes + plane) * send + slot, (slots, slots))
     scaled = (hidden_ref[...].astype(jnp.float32) * scale).astype(jnp.bfloat16)
     out_ref[...] = moved(scaled, source)
@@ -50,14 +52,13 @@
         pltpu.make_async_copy(weight_ref.at[:, i * block : (i + 1) * block], weights.at[i], in_sems.at[i])
         for i in range(pieces)
     ]
-    stores = [
-        pltpu.make_async_copy(outs.at[:, i * per : (i + 1) * per], out_ref.at[:, i * per : (i + 1) * per], out_sems.at[i])
-        for i in range(pieces)
-    ]
+    homes = [i * STRIDE % planes for i in range(planes)]
+    stores = [pltpu.make_async_copy(outs.at[:, i], out_ref.at[:, i], out_sems.at[i]) for i in homes]
     for load in loads:
         load.start()
     place = lax.broadcasted_iota(jnp.int32, (count, 1), 0)
     mate, group, slot = place // (planes * send), (place // send) % planes, place % send
+    group = group * STRIDE % planes
     source = jnp.broadcast_to((group * mates + mate) * send + slot, (count, count))
     rows = moved(rows_ref[...], source)
     bundle = planes * send
@@ -66,10 +67,11 @@
         product = jnp.dot(rows, weights[i], preferred_element_type=jnp.float32).astype(jnp.bfloat16)
         for j in range(per):
             for k in range(mates):
-                outs[k, i * per + j] = product[k * bundle : (k + 1) * bundle, j * strip : (j + 1) * strip]
-        if i:
-            stores[i - 1].start()
-    stores[-1].start()
+                outs[k, homes[i * per + j]] = product[k * bundle : (k + 1) * bundle, j * strip : (j + 1) * strip]
+        for store in stores[(i - 1) * per : i * per] if i else ():
+            store.start()
+    for store in stores[-per:]:
+        store.start()
     for store in stores:
         store.wait()
 
@@ -90,7 +92,7 @@
             pltpu.VMEM((pieces, depth, block), jnp.bfloat16),
             pltpu.VMEM(shape, jnp.bfloat16),
             pltpu.SemaphoreType.DMA((pieces,)),
-            pltpu.SemaphoreType.DMA((pieces,)),
+            pltpu.SemaphoreType.DMA((planes,)),
         ],
         cost_estimate=pl.CostEstimate(
             flops=2 * count * depth * width, bytes_accessed=2 * (depth + count) * width, transcendentals=0
@@ -122,7 +124,7 @@
     strip = width // planes
 
     rows = scaled_rows(hidden[0, 0], slot_gate[0], block_count[0], planes, mates, send)
-    rows = exchange(rows, "grp")
+    rows = exchange(rows, "grp", [[i * pow(STRIDE, -1, planes) % planes for i in range(planes)]])
 
     near = min(8, columns // 2)
     index = slot_owner[0, 0] * TOK_DEV + slot_row[0, 0]
@@ -143,12 +145,14 @@
     order = tuple(range(bits + 1, 1, -1)) + (0, 1, bits + 2)
     index = index.transpose(order).reshape(-1)
 
-    wanted = jnp.arange(planes * TOK_DEV)
+    order = [i * STRIDE % planes for i in range(planes)]
+    place = jnp.arange(planes) * STRIDE % planes
+    wanted = (place[:, None] * TOK_DEV + jnp.arange(TOK_DEV)[None, :]).reshape(-1)
     table = (wanted[:, None] == index[None, :]).astype(jnp.bfloat16)
     summed = jnp.dot(table, arrived, preferred_element_type=jnp.float32).astype(jnp.bfloat16)
 
-    summed = exchange(summed, "grp")
-    siblings = [[mate * planes + d for d in range(planes)] for mate in range(mates)]
+    summed = exchange(summed, "grp", [order])
+    siblings = [[mate * planes + d for d in order] for mate in range(mates)]
     summed = exchange(summed, "ep", siblings)
     return summed.reshape(planes, TOK_DEV, strip).swapaxes(0, 1).reshape(TOK_DEV, width)
 

time: 158 us -> 156 us (0.987)
  no operation moved by 1% of the time
where the time goes in v7:
time: 156 us
  blocking collectives  81.3 us (52%)
  starting transfers between devices  49.8 us (32%)
  waiting for transfers between devices  12.8 us (8%)
  Pallas kernels  8.23 us (5%)
  local copies, waits for them, and re-layouts  2.16 us (1%)
    all_to_all x2, blocking collectives, exchange(): lax.all_to_all(value, axis, split_axis=0, concat_axis=0, tiled=True, axis...  36.9 us
    all_to_all x2, starting transfers between devices, exchange(): lax.all_to_all(value, axis, split_axis=0, concat_axis=0, tiled=True, axis...  35.3 us
    all_gather x1, blocking collectives, body(): index = lax.all_gather(index, 'grp', axis=0)  26 us
    all_gather x1, blocking collectives, body(): index = lax.all_gather(index, 'ep', axis=0, axis_index_groups=groups)  18.4 us
    ppermute x3, starting transfers between devices, doubled(): other = lax.ppermute(index, 'ep', [(i, i ^ step) for i in range(columns)])  14.5 us
    all_to_all x2, waiting for transfers between devices, exchange(): lax.all_to_all(value, axis, split_axis=0, concat_axis=0, tiled=True, axis...  8.8 us
    pallas_call x1, Pallas kernels, strip_product(): pl.pallas_call(lambda *refs: product_kernel(planes, mates, send, *refs),...  5.86 us
    ppermute x3, waiting for transfers between devices, doubled(): other = lax.ppermute(index, 'ep', [(i, i ^ step) for i in range(columns)])  3.96 us
  transfers between devices with their start and end apart: 5, of which 5 were waited for; matrix products, arithmetic and copies ran while one was open for 1% of the time, Pallas kernels for 0%

profile of v7, /device:TPU:1, one launch (start us, length us, event | category | flops | bytes accessed | tf_op | source)
XLA Modules:
  0.0 155.9 jit_solution(17858101457122387400)
XLA Ops:
  0.0 2.4 %scaled_rows.1 = bf16[256,1024]{1,0:T(8,128)(2,1)} custom-call(f32[1,256]{1,0:T(1,128)} %bitcast.51, s32[1,64]{1,0:T(1,128)} %bitcast.52, bf16[256,1024]{1,0:T(8,128)(2,1)} %bitcast.41), custom_call_target="tpu_custom_call" | custom-call | flops 524288 | bytes 1048576 | tf_op jit(solution)/shard_map/scaled_rows/pallas_call | solution.py:38
  2.4 19.4 %all-to-all-start = ((bf16[16,16,1024]{2,1,0:T(8,128)(2,1)}), bf16[16,16,1024]{2,1,0:T(8,128)(2,1)S(1)}, u32[]{:S(2)}, u32[]{:S(2)}) async-start(bf16[16,16,1024]{2,1,0:T(8,128)(2,1)} %bitcast.38), calls=%async_computation | async-start | bytes 1048576 | tf_op jit(solution)/shard_map/all_to_all | solution.py:13
  21.8 7.5 %collective-permute-start = (s32[256]{0:T(256)S(1)}, s32[256]{0:T(256)S(1)}, u32[]{:S(2)}, u32[]{:S(2)}) collective-permute-start(s32[256]{0:T(256)S(1)} %bitcast.49), channel_id=1, source_target_pairs={{0,32},{1,33},{2,34},{3,35},{4,36},{5,37},{6,38},{7,39},{8,40},{9,... | collective-permute-start | bytes 3080 | tf_op jit(solution)/shard_map/ppermute | solution.py:110
  29.3 0.9 collective-permute-done
  30.2 4.0 %collective-permute-start.1 = (s32[2,256]{1,0:T(2,128)S(1)}, s32[2,256]{1,0:T(2,128)S(1)}, u32[]{:S(2)}, u32[]{:S(2)}) collective-permute-start(s32[2,256]{1,0:T(2,128)S(1)} %pad_add_fusion.2), channel_id=1, source_target_pairs={{0,16},{1,17},{2,18},{3,19},{4,20},{5,21},{6,22},{7,23},{8,24},{9,... | collective-permute-start | bytes 6152 | tf_op jit(solution)/shard_map/ppermute | solution.py:110
  34.3 1.5 collective-permute-done.1
  35.8 3.0 %collective-permute-start.2 = (s32[2,2,256]{2,1,0:T(2,128)S(1)}, s32[2,2,256]{2,1,0:T(2,128)S(1)}, u32[]{:S(2)}, u32[]{:S(2)}) collective-permute-start(s32[2,2,256]{2,1,0:T(2,128)S(1)} %pad_add_fusion.1), channel_id=1, source_target_pairs={{0,8},{1,9},{2,10},{3,11},{4,12},{5,13},{6,14},{7,15},{8,0},{9,1},... | collective-permute-start | bytes 12296 | tf_op jit(solution)/shard_map/ppermute | solution.py:110
  38.8 1.6 %collective-permute-done.2 = s32[2,2,256]{2,1,0:T(2,128)S(1)} collective-permute-done((s32[2,2,256]{2,1,0:T(2,128)S(1)}, s32[2,2,256]{2,1,0:T(2,128)S(1)}, u32[]{:S(2)}, u32[]{:S(2)}) %collective-permute-start.2) | collective-permute-done | bytes 4128 | tf_op jit(solution)/shard_map/ppermute | solution.py:110
  40.4 0.3 reshape.61
  40.7 0.1 copy.18
  40.9 4.6 %all-to-all-done = bf16[16,16,1024]{2,1,0:T(8,128)(2,1)S(1)} async-done(((bf16[16,16,1024]{2,1,0:T(8,128)(2,1)}), bf16[16,16,1024]{2,1,0:T(8,128)(2,1)S(1)}, u32[]{:S(2)}, u32[]{:S(2)}) %all-to-all-start) | async-done | bytes 524320 | tf_op jit(solution)/shard_map/all_to_all | solution.py:13
  45.5 5.9 %strip_product.1 = bf16[4,16,64,256]{3,2,1,0:T(8,128)(2,1)} custom-call(bf16[256,1024]{1,0:T(8,128)(2,1)S(1)} %bitcast.35, bf16[1024,4096]{1,0:T(8,128)(2,1)} %bitcast.36), custom_call_target="tpu_custom_call" | custom-call | flops 2147483648 | bytes 10485760 | tf_op jit(solution)/shard_map/strip_product/pallas_call | solution.py:86
  51.4 15.9 %all-to-all-start.1 = ((bf16[64,64,256]{2,1,0:T(8,128)(2,1)}), bf16[64,64,256]{2,1,0:T(8,128)(2,1)S(1)}, u32[]{:S(2)}, u32[]{:S(2)}) async-start(bf16[64,64,256]{2,1,0:T(8,128)(2,1)} %bitcast.19), calls=%async_computation.1 | async-start | bytes 4194304 | tf_op jit(solution)/shard_map/all_to_all | solution.py:13
  67.3 0.1 add.61
  67.5 26.0 %all-gather = s32[256,32]{1,0:T(8,128)S(1)} all-gather(s32[16,32]{1,0:T(8,128)S(1)} %copy.19), channel_id=2, replica_groups=mesh['grp'=16,'ep'=64] {'grp'}, dimensions={0}, use_global_device_ids=true | all-gather | bytes 34816 | tf_op jit(solution)/shard_map/all_gather | solution.py:140
  93.5 18.4 %all-gather.1 = s32[128,1,32]{2,1,0:T(1,128)S(1)} all-gather(s32[16,1,32]{2,1,0:T(1,128)S(1)} %constant_dynamic-slice_fusion), channel_id=3, replica_groups={{0,1,2,3,4,5,6,7},{8,9,10,11,12,13,14,15},{16,17,18,19,20,21,22,23},{24..., dimensions={0}, use_global_device_ids=true | all-gather | bytes 18432 | tf_op jit(solution)/shard_map/all_gather | solution.py:143
  111.9 0.1 reshape.63
  112.1 0.4 copy.21
  112.5 0.3 eq.34
  112.8 4.2 %all-to-all-done.1 = bf16[64,64,256]{2,1,0:T(8,128)(2,1)S(1)} async-done(((bf16[64,64,256]{2,1,0:T(8,128)(2,1)}), bf16[64,64,256]{2,1,0:T(8,128)(2,1)S(1)}, u32[]{:S(2)}, u32[]{:S(2)}) %all-to-all-start.1) | async-done | bytes 2097184 | tf_op jit(solution)/shard_map/all_to_all | solution.py:13
  116.9 1.3 fusion.4
  118.3 19.3 %all_to_all.39 = bf16[16,32,256]{2,1,0:T(8,128)(2,1)S(1)} all-to-all(bf16[16,32,256]{2,1,0:T(8,128)(2,1)S(1)} %bitcast.42), channel_id=1, replica_groups={{0,192,384,576,768,960,128,320,512,704,896,64,256,448,640,832},{1,193,3..., dimensions={0} | all-to-all | bytes 524288 | tf_op jit(solution)/shard_map/all_to_all | solution.py:13
  137.5 17.7 %all_to_all.40 = bf16[16,32,256]{2,1,0:T(8,128)(2,1)S(1)} all-to-all(bf16[16,32,256]{2,1,0:T(8,128)(2,1)S(1)} %all_to_all.39), channel_id=1, replica_groups={{0,3,6,9,12,15,2,5,8,11,14,1,4,7,10,13},{16,19,22,25,28,31,18,21,24,27,..., dimensions={0} | all-to-all | bytes 524288 | tf_op jit(solution)/shard_map/all_to_all | solution.py:13
  155.2 0.7 copy.24
  (17 shorter events, 0.3 us)
Async XLA Ops:
  0.0 21.8 %copy-start = (s32[1,1,256]{2,1,0:T(1,128)S(1)}, s32[1,1,256]{2,1,0:T(1,128)}, u32[]{:S(2)}) copy-start(s32[1,1,256]{2,1,0:T(1,128)} %param.10) | copy-start | bytes 3076
  0.0 21.8 %copy-start.1 = (s32[1,1,256]{2,1,0:T(1,128)S(1)}, s32[1,1,256]{2,1,0:T(1,128)}, u32[]{:S(2)}) copy-start(s32[1,1,256]{2,1,0:T(1,128)} %param.9) | copy-start | bytes 3076
  2.4 43.1 %all-to-all-start = ((bf16[16,16,1024]{2,1,0:T(8,128)(2,1)}), bf16[16,16,1024]{2,1,0:T(8,128)(2,1)S(1)}, u32[]{:S(2)}, u32[]{:S(2)}) async-start(bf16[16,16,1024]{2,1,0:T(8,128)(2,1)} %bitcast.38), calls=%async_computation | async-start | bytes 1048576 | tf_op jit(solution)/shard_map/all_to_all | solution.py:13
  21.8 8.4 %collective-permute-start = (s32[256]{0:T(256)S(1)}, s32[256]{0:T(256)S(1)}, u32[]{:S(2)}, u32[]{:S(2)}) collective-permute-start(s32[256]{0:T(256)S(1)} %bitcast.49), channel_id=1, source_target_pairs={{0,32},{1,33},{2,34},{3,35},{4,36},{5,37},{6,38},{7,39},{8,40},{9,... | collective-permute-start | bytes 3080 | tf_op jit(solution)/shard_map/ppermute | solution.py:110
  30.2 5.5 %collective-permute-start.1 = (s32[2,256]{1,0:T(2,128)S(1)}, s32[2,256]{1,0:T(2,128)S(1)}, u32[]{:S(2)}, u32[]{:S(2)}) collective-permute-start(s32[2,256]{1,0:T(2,128)S(1)} %pad_add_fusion.2), channel_id=1, source_target_pairs={{0,16},{1,17},{2,18},{3,19},{4,20},{5,21},{6,22},{7,23},{8,24},{9,... | collective-permute-start | bytes 6152 | tf_op jit(solution)/shard_map/ppermute | solution.py:110
  35.8 4.6 %collective-permute-start.2 = (s32[2,2,256]{2,1,0:T(2,128)S(1)}, s32[2,2,256]{2,1,0:T(2,128)S(1)}, u32[]{:S(2)}, u32[]{:S(2)}) collective-permute-start(s32[2,2,256]{2,1,0:T(2,128)S(1)} %pad_add_fusion.1), channel_id=1, source_target_pairs={{0,8},{1,9},{2,10},{3,11},{4,12},{5,13},{6,14},{7,15},{8,0},{9,1},... | collective-permute-start | bytes 12296 | tf_op jit(solution)/shard_map/ppermute | solution.py:110
  51.4 65.6 %all-to-all-start.1 = ((bf16[64,64,256]{2,1,0:T(8,128)(2,1)}), bf16[64,64,256]{2,1,0:T(8,128)(2,1)S(1)}, u32[]{:S(2)}, u32[]{:S(2)}) async-start(bf16[64,64,256]{2,1,0:T(8,128)(2,1)} %bitcast.19), calls=%async_computation.1 | async-start | bytes 4194304 | tf_op jit(solution)/shard_map/all_to_all | solution.py:13

commit v8 on v7

--- a/solution.py
+++ b/solution.py
@@ -6,7 +6,7 @@
 from jax.sharding import PartitionSpec as P
 
 TOK_DEV = 32
-STRIDE = 3
+STRIDE = 11
 
 
 def exchange(value, axis, groups=None):
@@ -27,7 +27,7 @@
     block = slot // send == lax.broadcasted_iota(jnp.int32, (slots, columns), 1)
     limit = jnp.sum(jnp.where(block, count_ref[...], 0).astype(jnp.float32), axis=1, keepdims=True)
     scale = jnp.where((slot % send).astype(jnp.float32) < limit, gate, 0.0)
-    plane = slot // (mates * send) * pow(STRIDE, -1, planes) % planes
+    plane = slot // (mates * send) * STRIDE % planes
     mate, slot = (slot // send) % mates, slot % send
     source = jnp.broadcast_to((mate * planes + plane) * send + slot, (slots, slots))
     scaled = (hidden_ref[...].astype(jnp.float32) * scale).astype(jnp.bfloat16)
@@ -52,13 +52,12 @@
         pltpu.make_async_copy(weight_ref.at[:, i * block : (i + 1) * block], weights.at[i], in_sems.at[i])
         for i in range(pieces)
     ]
-    homes = [i * STRIDE % planes for i in range(planes)]
-    stores = [pltpu.make_async_copy(outs.at[:, i], out_ref.at[:, i], out_sems.at[i]) for i in homes]
+    stores = [pltpu.make_async_copy(outs.at[:, i], out_ref.at[:, i], out_sems.at[i]) for i in range(planes)]
     for load in loads:
         load.start()
     place = lax.broadcasted_iota(jnp.int32, (count, 1), 0)
     mate, group, slot = place // (planes * send), (place // send) % planes, place % send
-    group = group * STRIDE % planes
+    group = group * pow(STRIDE, -1, planes) % planes
     source = jnp.broadcast_to((group * mates + mate) * send + slot, (count, count))
     rows = moved(rows_ref[...], source)
     bundle = planes * send
@@ -67,7 +66,7 @@
         product = jnp.dot(rows, weights[i], preferred_element_type=jnp.float32).astype(jnp.bfloat16)
         for j in range(per):
             for k in range(mates):
-                outs[k, homes[i * per + j]] = product[k * bundle : (k + 1) * bundle, j * strip : (j + 1) * strip]
+                outs[k, i * per + j] = product[k * bundle : (k + 1) * bundle, j * strip : (j + 1) * strip]
         for store in stores[(i - 1) * per : i * per] if i else ():
             store.start()
     for store in stores[-per:]:
@@ -80,7 +79,7 @@
     count, depth = rows.shape
     width = weight.shape[1]
     strip = width // planes
-    block = 2 * strip
+    block = 4 * strip
     pieces = width // block
     shape = (mates, planes, planes * send, strip)
     return pl.pallas_call(
@@ -124,7 +123,7 @@
     strip = width // planes
 
     rows = scaled_rows(hidden[0, 0], slot_gate[0], block_count[0], planes, mates, send)
-    rows = exchange(rows, "grp", [[i * pow(STRIDE, -1, planes) % planes for i in range(planes)]])
+    rows = exchange(rows, "grp", [[i * STRIDE % planes for i in range(planes)]])
 
     near = min(8, columns // 2)
     index = slot_owner[0, 0] * TOK_DEV + slot_row[0, 0]
@@ -145,14 +144,12 @@
     order = tuple(range(bits + 1, 1, -1)) + (0, 1, bits + 2)
     index = index.transpose(order).reshape(-1)
 
-    order = [i * STRIDE % planes for i in range(planes)]
-    place = jnp.arange(planes) * STRIDE % planes
-    wanted = (place[:, None] * TOK_DEV + jnp.arange(TOK_DEV)[None, :]).reshape(-1)
+    wanted = jnp.arange(planes * TOK_DEV)
     table = (wanted[:, None] == index[None, :]).astype(jnp.bfloat16)
     summed = jnp.dot(table, arrived, preferred_element_type=jnp.float32).astype(jnp.bfloat16)
 
-    summed = exchange(summed, "grp", [order])
-    siblings = [[mate * planes + d for d in order] for mate in range(mates)]
+    summed = exchange(summed, "grp")
+    siblings = [[mate * planes + d for d in range(planes)] for mate in range(mates)]
     summed = exchange(summed, "ep", siblings)
     return summed.reshape(planes, TOK_DEV, strip).swapaxes(0, 1).reshape(TOK_DEV, width)
 

time: 156 us -> 158 us (1.013)
  no operation moved by 1% of the time
where the time goes in v8:
time: 158 us; the launch traced here: 157 us
  blocking collectives  82.7 us (52%)
  starting transfers between devices  49.8 us (32%)
  waiting for transfers between devices  12.9 us (8%)
  Pallas kernels  8.09 us (5%)
  local copies, waits for them, and re-layouts  2.08 us (1%)
    all_to_all x2, blocking collectives, exchange(): lax.all_to_all(value, axis, split_axis=0, concat_axis=0, tiled=True, axis...  38.3 us
    all_to_all x2, starting transfers between devices, exchange(): lax.all_to_all(value, axis, split_axis=0, concat_axis=0, tiled=True, axis...  35.3 us
    all_gather x1, blocking collectives, body(): index = lax.all_gather(index, 'grp', axis=0)  26 us
    all_gather x1, blocking collectives, body(): index = lax.all_gather(index, 'ep', axis=0, axis_index_groups=groups)  18.4 us
    ppermute x3, starting transfers between devices, doubled(): other = lax.ppermute(index, 'ep', [(i, i ^ step) for i in range(columns)])  14.5 us
    all_to_all x2, waiting for transfers between devices, exchange(): lax.all_to_all(value, axis, split_axis=0, concat_axis=0, tiled=True, axis...  8.96 us
    pallas_call x1, Pallas kernels, strip_product(): pl.pallas_call(lambda *refs: product_kernel(planes, mates, send, *refs),...  5.72 us
    ppermute x3, waiting for transfers between devices, doubled(): other = lax.ppermute(index, 'ep', [(i, i ^ step) for i in range(columns)])  3.96 us
  transfers between devices with their start and end apart: 5, of which 5 were waited for; matrix products, arithmetic and copies ran while one was open for 1% of the time, Pallas kernels for 0%

profile of v8, /device:TPU:1, one launch (start us, length us, event | category | flops | bytes accessed | tf_op | source)
XLA Modules:
  0.0 157.2 jit_solution(4390012427618772726)
XLA Ops:
  0.0 2.4 %scaled_rows.1 = bf16[256,1024]{1,0:T(8,128)(2,1)} custom-call(f32[1,256]{1,0:T(1,128)} %bitcast.51, s32[1,64]{1,0:T(1,128)} %bitcast.52, bf16[256,1024]{1,0:T(8,128)(2,1)} %bitcast.41), custom_call_target="tpu_custom_call" | custom-call | flops 524288 | bytes 1048576 | tf_op jit(solution)/shard_map/scaled_rows/pallas_call | solution.py:38
  2.4 19.4 %all-to-all-start = ((bf16[16,16,1024]{2,1,0:T(8,128)(2,1)}), bf16[16,16,1024]{2,1,0:T(8,128)(2,1)S(1)}, u32[]{:S(2)}, u32[]{:S(2)}) async-start(bf16[16,16,1024]{2,1,0:T(8,128)(2,1)} %bitcast.38), calls=%async_computation | async-start | bytes 1048576 | tf_op jit(solution)/shard_map/all_to_all | solution.py:13
  21.8 7.5 %collective-permute-start = (s32[256]{0:T(256)S(1)}, s32[256]{0:T(256)S(1)}, u32[]{:S(2)}, u32[]{:S(2)}) collective-permute-start(s32[256]{0:T(256)S(1)} %bitcast.49), channel_id=1, source_target_pairs={{0,32},{1,33},{2,34},{3,35},{4,36},{5,37},{6,38},{7,39},{8,40},{9,... | collective-permute-start | bytes 3080 | tf_op jit(solution)/shard_map/ppermute | solution.py:109
  29.3 0.9 collective-permute-done
  30.2 4.0 %collective-permute-start.1 = (s32[2,256]{1,0:T(2,128)S(1)}, s32[2,256]{1,0:T(2,128)S(1)}, u32[]{:S(2)}, u32[]{:S(2)}) collective-permute-start(s32[2,256]{1,0:T(2,128)S(1)} %pad_add_fusion.2), channel_id=1, source_target_pairs={{0,16},{1,17},{2,18},{3,19},{4,20},{5,21},{6,22},{7,23},{8,24},{9,... | collective-permute-start | bytes 6152 | tf_op jit(solution)/shard_map/ppermute | solution.py:109
  34.3 1.5 collective-permute-done.1
  35.8 3.0 %collective-permute-start.2 = (s32[2,2,256]{2,1,0:T(2,128)S(1)}, s32[2,2,256]{2,1,0:T(2,128)S(1)}, u32[]{:S(2)}, u32[]{:S(2)}) collective-permute-start(s32[2,2,256]{2,1,0:T(2,128)S(1)} %pad_add_fusion.1), channel_id=1, source_target_pairs={{0,8},{1,9},{2,10},{3,11},{4,12},{5,13},{6,14},{7,15},{8,0},{9,1},... | collective-permute-start | bytes 12296 | tf_op jit(solution)/shard_map/ppermute | solution.py:109
  38.8 1.6 %collective-permute-done.2 = s32[2,2,256]{2,1,0:T(2,128)S(1)} collective-permute-done((s32[2,2,256]{2,1,0:T(2,128)S(1)}, s32[2,2,256]{2,1,0:T(2,128)S(1)}, u32[]{:S(2)}, u32[]{:S(2)}) %collective-permute-start.2) | collective-permute-done | bytes 4128 | tf_op jit(solution)/shard_map/ppermute | solution.py:109
  40.4 0.3 reshape.30
  40.7 0.1 copy.18
  40.9 4.6 %all-to-all-done = bf16[16,16,1024]{2,1,0:T(8,128)(2,1)S(1)} async-done(((bf16[16,16,1024]{2,1,0:T(8,128)(2,1)}), bf16[16,16,1024]{2,1,0:T(8,128)(2,1)S(1)}, u32[]{:S(2)}, u32[]{:S(2)}) %all-to-all-start) | async-done | bytes 524320 | tf_op jit(solution)/shard_map/all_to_all | solution.py:13
  45.5 5.7 %strip_product.1 = bf16[4,16,64,256]{3,2,1,0:T(8,128)(2,1)} custom-call(bf16[256,1024]{1,0:T(8,128)(2,1)S(1)} %bitcast.35, bf16[1024,4096]{1,0:T(8,128)(2,1)} %bitcast.36), custom_call_target="tpu_custom_call" | custom-call | flops 2147483648 | bytes 10485760 | tf_op jit(solution)/shard_map/strip_product/pallas_call | solution.py:85
  51.2 15.9 %all-to-all-start.1 = ((bf16[64,64,256]{2,1,0:T(8,128)(2,1)}), bf16[64,64,256]{2,1,0:T(8,128)(2,1)S(1)}, u32[]{:S(2)}, u32[]{:S(2)}) async-start(bf16[64,64,256]{2,1,0:T(8,128)(2,1)} %bitcast.19), calls=%async_computation.1 | async-start | bytes 4194304 | tf_op jit(solution)/shard_map/all_to_all | solution.py:13
  67.1 0.1 copy.19
  67.2 26.0 %all-gather = s32[256,32]{1,0:T(8,128)S(1)} all-gather(s32[16,32]{1,0:T(8,128)S(1)} %copy.19), channel_id=2, replica_groups=mesh['grp'=16,'ep'=64] {'grp'}, dimensions={0}, use_global_device_ids=true | all-gather | bytes 34816 | tf_op jit(solution)/shard_map/all_gather | solution.py:139
  93.1 18.4 %all-gather.1 = s32[128,1,32]{2,1,0:T(1,128)S(1)} all-gather(s32[16,1,32]{2,1,0:T(1,128)S(1)} %constant_dynamic-slice_fusion), channel_id=3, replica_groups={{0,1,2,3,4,5,6,7},{8,9,10,11,12,13,14,15},{16,17,18,19,20,21,22,23},{24..., dimensions={0}, use_global_device_ids=true | all-gather | bytes 18432 | tf_op jit(solution)/shard_map/all_gather | solution.py:142
  111.6 0.1 reshape.32
  111.7 0.4 copy.21
  112.2 0.3 eq.32
  112.5 4.3 %all-to-all-done.1 = bf16[64,64,256]{2,1,0:T(8,128)(2,1)S(1)} async-done(((bf16[64,64,256]{2,1,0:T(8,128)(2,1)}), bf16[64,64,256]{2,1,0:T(8,128)(2,1)S(1)}, u32[]{:S(2)}, u32[]{:S(2)}) %all-to-all-start.1) | async-done | bytes 2097184 | tf_op jit(solution)/shard_map/all_to_all | solution.py:13
  116.8 1.4 fusion.2
  118.2 19.1 %all_to_all.39 = bf16[16,32,256]{2,1,0:T(8,128)(2,1)S(1)} all-to-all(bf16[16,32,256]{2,1,0:T(8,128)(2,1)S(1)} %bitcast.42), channel_id=1, replica_groups=mesh['grp'=16,'ep'=64] {'grp'}, dimensions={0} | all-to-all | bytes 524288 | tf_op jit(solution)/shard_map/all_to_all | solution.py:13
  137.3 19.2 %all_to_all.40 = bf16[16,32,256]{2,1,0:T(8,128)(2,1)S(1)} all-to-all(bf16[16,32,256]{2,1,0:T(8,128)(2,1)S(1)} %all_to_all.39), channel_id=1, replica_groups={{0,1,2,3,4,5,6,7,8,9,10,11,12,13,14,15},{16,17,18,19,20,21,22,23,24,25,..., dimensions={0} | all-to-all | bytes 524288 | tf_op jit(solution)/shard_map/all_to_all | solution.py:13
  156.5 0.7 copy.24
  (14 shorter events, 0.1 us)
Async XLA Ops:
  0.0 21.8 %copy-start = (s32[1,1,256]{2,1,0:T(1,128)S(1)}, s32[1,1,256]{2,1,0:T(1,128)}, u32[]{:S(2)}) copy-start(s32[1,1,256]{2,1,0:T(1,128)} %param.10) | copy-start | bytes 3076
  0.0 21.8 %copy-start.1 = (s32[1,1,256]{2,1,0:T(1,128)S(1)}, s32[1,1,256]{2,1,0:T(1,128)}, u32[]{:S(2)}) copy-start(s32[1,1,256]{2,1,0:T(1,128)} %param.9) | copy-start | bytes 3076
  2.4 43.1 %all-to-all-start = ((bf16[16,16,1024]{2,1,0:T(8,128)(2,1)}), bf16[16,16,1024]{2,1,0:T(8,128)(2,1)S(1)}, u32[]{:S(2)}, u32[]{:S(2)}) async-start(bf16[16,16,1024]{2,1,0:T(8,128)(2,1)} %bitcast.38), calls=%async_computation | async-start | bytes 1048576 | tf_op jit(solution)/shard_map/all_to_all | solution.py:13
  21.8 8.4 %collective-permute-start = (s32[256]{0:T(256)S(1)}, s32[256]{0:T(256)S(1)}, u32[]{:S(2)}, u32[]{:S(2)}) collective-permute-start(s32[256]{0:T(256)S(1)} %bitcast.49), channel_id=1, source_target_pairs={{0,32},{1,33},{2,34},{3,35},{4,36},{5,37},{6,38},{7,39},{8,40},{9,... | collective-permute-start | bytes 3080 | tf_op jit(solution)/shard_map/ppermute | solution.py:109
  30.2 5.5 %collective-permute-start.1 = (s32[2,256]{1,0:T(2,128)S(1)}, s32[2,256]{1,0:T(2,128)S(1)}, u32[]{:S(2)}, u32[]{:S(2)}) collective-permute-start(s32[2,256]{1,0:T(2,128)S(1)} %pad_add_fusion.2), channel_id=1, source_target_pairs={{0,16},{1,17},{2,18},{3,19},{4,20},{5,21},{6,22},{7,23},{8,24},{9,... | collective-permute-start | bytes 6152 | tf_op jit(solution)/shard_map/ppermute | solution.py:109
  35.8 4.6 %collective-permute-start.2 = (s32[2,2,256]{2,1,0:T(2,128)S(1)}, s32[2,2,256]{2,1,0:T(2,128)S(1)}, u32[]{:S(2)}, u32[]{:S(2)}) collective-permute-start(s32[2,2,256]{2,1,0:T(2,128)S(1)} %pad_add_fusion.1), channel_id=1, source_target_pairs={{0,8},{1,9},{2,10},{3,11},{4,12},{5,13},{6,14},{7,15},{8,0},{9,1},... | collective-permute-start | bytes 12296 | tf_op jit(solution)/shard_map/ppermute | solution.py:109
  51.2 65.6 %all-to-all-start.1 = ((bf16[64,64,256]{2,1,0:T(8,128)(2,1)}), bf16[64,64,256]{2,1,0:T(8,128)(2,1)S(1)}, u32[]{:S(2)}, u32[]{:S(2)}) async-start(bf16[64,64,256]{2,1,0:T(8,128)(2,1)} %bitcast.19), calls=%async_computation.1 | async-start | bytes 4194304 | tf_op jit(solution)/shard_map/all_to_all | solution.py:13
